TPU v7x, 32 devices: a whole 2x2x4 slice. The times are simulated.
32 devices in a mesh: batch: 4 (over y, x), heads: 8 (over z, core).
Axes of the slice: x: 2, y: 2, z: 4, core: 2. Of those that a mesh axis runs over, the one named last changes fastest.
Arguments:
- draft_ids: int32 [192, 8], P('batch'), may hold values from 0 to 50279
- accepted: int32 [192], P('batch'), may hold values from 1 to 8
- embedding: bfloat16 [50280, 2560], P(None, 'heads'), may hold values from -6 to 6
- norm_gain: float32 [2, 2560], replicated, may hold values from 0.5 to 1.5
- w_zx: bfloat16 [2, 2560, 8, 128], P(None, None, 'heads'), may hold values from -0.125 to 0.125
- w_dt: bfloat16 [2, 2560, 8], P(None, None, 'heads'), may hold values from -0.125 to 0.125
- w_bc: bfloat16 [2, 2560, 256], P(None, None, 'heads'), may hold values from -0.125 to 0.125
- dt_bias: float32 [2, 8], P(None, 'heads'), may hold values from -4 to -1
- decay_rate: float32 [2, 8], P(None, 'heads'), may hold values from 1 to 16
- skip_weight: float32 [2, 8], P(None, 'heads'), may hold values from 0.5 to 1.5
- conv_x_w: bfloat16 [2, 4, 512], P(None, None, 'heads'), may hold values from -3 to 3
- conv_x_b: bfloat16 [2, 512], P(None, 'heads'), may hold values from -3 to 3
- conv_bc_w: bfloat16 [2, 4, 256], P(None, None, 'heads'), may hold values from -3 to 3
- conv_bc_b: bfloat16 [2, 256], P(None, 'heads'), may hold values from -3 to 3
- gate_gain: float32 [2, 512], P(None, 'heads'), may hold values from 0.5 to 1.5
- out_w: bfloat16 [2, 512, 2560], P(None, 'heads'), may hold values from -0.375 to 0.375
- ssm_state: float32 [2, 192, 8, 64, 128], P(None, 'batch', 'heads'), may hold values from -1.6 to 1.6
- conv_x_state: bfloat16 [2, 192, 3, 512], P(None, 'batch', None, 'heads'), may hold values from -6 to 6
- conv_bc_state: bfloat16 [2, 192, 3, 256], P(None, 'batch', None, 'heads'), may hold values from -6 to 6
Outputs:
- hidden_out: bfloat16 [1536, 2560], P('batch', 'heads')
- new_ssm: float32 [2, 192, 8, 64, 128], P(None, 'batch', 'heads')
- new_conv_x: bfloat16 [2, 192, 3, 512], P(None, 'batch', None, 'heads')
- new_conv_bc: bfloat16 [2, 192, 3, 256], P(None, 'batch', None, 'heads')
Inputs may be any that keep to these rules, and one draw needn't show every extreme that they name: `accepted`: the number of a sequence's draft tokens that are kept, counted from the first.
All inputs are finite; a program needn't handle non-finite values.
Results may differ from a plain program's by a relative error of at most 0.015.
Values may be sent and summed in bfloat16 or wider, within the bound.
A program may use at most 128 MiB of HBM per device.

v0:
```python
import functools

import jax
import jax.numpy as jnp
from jax import lax
from jax.experimental import pallas as pl
from jax.experimental.pallas import tpu as pltpu
from jax.sharding import PartitionSpec as P

LAYERS = 2
EPS = 1e-05
MESH = pl.DeviceIdType.MESH
CHUNK = 2048
VMEM_LIMIT = 60 * 1024 * 1024


def rms_scale(total, count):
    return lax.rsqrt(total / count + EPS)


def dot_tn(a, b):
    return lax.dot_general(a, b, (((0,), (0,)), ((), ())), preferred_element_type=jnp.float32)


def dot_nt(a, b):
    return lax.dot_general(a, b, (((1,), (1,)), ((), ())), preferred_element_type=jnp.float32)


def keep_rows(window, accepted, kept_rows):
    last_start = window.shape[1] - kept_rows
    kept = window[:, 1 : 1 + kept_rows]
    for start in range(2, last_start + 1):
        kept = jnp.where(
            (accepted == start)[:, None, None], window[:, start : start + kept_rows], kept
        )
    return kept


def greet(n):
    me = lax.axis_index("heads")
    barrier = pltpu.get_barrier_semaphore()
    for d in range(1, n):
        pl.semaphore_signal(
            barrier, inc=1, device_id={"heads": lax.rem(me + d, n)}, device_id_type=MESH
        )
    pl.semaphore_wait(barrier, n - 1)


class Gather:
    def __init__(self, n, src, out, send, recv, fsend, frecv):
        self.n, self.src, self.out = n, src, out
        self.send, self.recv, self.fsend, self.frecv = send, recv, fsend, frecv
        self.me = lax.axis_index("heads")
        self.core = lax.rem(self.me, 2)
        self.chip = self.me // 2
        self.chips = n // 2
        self.mate = self.me + 1 - 2 * self.core

    def slot(self, c, core):
        return 2 * lax.rem(self.chip + self.chips - c, self.chips) + core

    def copy(self, src, slot, device, send, recv):
        return pltpu.make_async_remote_copy(
            src_ref=src,
            dst_ref=self.out.at[slot],
            send_sem=send,
            recv_sem=recv,
            device_id={"heads": device},
            device_id_type=MESH,
        )

    def first(self, c):
        if c == 0:
            return self.copy(self.src, self.me, self.mate, self.send.at[0], self.recv.at[0])
        dst = 2 * lax.rem(self.chip + c, self.chips) + self.core
        return self.copy(self.src, self.me, dst, self.send.at[c], self.recv.at[c])

    def arrival(self, c):
        if c == 0:
            return self.copy(self.src, self.mate, self.mate, self.send.at[0], self.recv.at[0])
        slot = self.slot(c, self.core)
        return self.copy(self.src, slot, slot, self.send.at[c], self.recv.at[c])

    def forward(self, c):
        slot = self.slot(c, self.core)
        return self.copy(
            self.out.at[slot], slot, self.mate, self.fsend.at[c], self.frecv.at[c]
        )

    def forwarded(self, c):
        slot = self.slot(c, 1 - self.core)
        return self.copy(
            self.out.at[slot], slot, self.mate, self.fsend.at[c], self.frecv.at[c]
        )

    def order(self):
        return sorted(range(1, self.chips), key=lambda c: min(c, self.chips - c))

    def start(self):
        for c in self.order():
            self.first(c).start()
        self.first(0).start()

    def relay(self):
        for c in self.order():
            self.arrival(c).wait_recv()
            self.forward(c).start()

    def finish(self):
        for c in range(self.chips):
            self.first(c).wait_send()
        self.arrival(0).wait_recv()
        for c in range(1, self.chips):
            self.forwarded(c).wait_recv()
            self.forward(c).wait_send()


def gather_sems(n, count):
    return [pltpu.SemaphoreType.DMA((n // 2,))] * (4 * count)


def ag_kernel(n, count, *refs):
    srcs, outs = refs[:count], refs[count : 2 * count]
    sems, local = refs[2 * count : -1], refs[-1]
    greet(n)
    me = lax.axis_index("heads")
    gathers = [
        Gather(n, srcs[i], outs[i], *sems[4 * i : 4 * i + 4]) for i in range(count)
    ]
    owns = [
        pltpu.make_async_copy(srcs[i], outs[i].at[me], local.at[i]) for i in range(count)
    ]
    for g in gathers:
        g.start()
    for own in owns:
        own.start()
    for g in gathers:
        g.relay()
    for g in gathers:
        g.finish()
    for own in owns:
        own.wait()


def all_gather(arrays, n, cid):
    count = len(arrays)
    return pl.pallas_call(
        functools.partial(ag_kernel, n, count),
        out_shape=[jax.ShapeDtypeStruct((n,) + a.shape, a.dtype) for a in arrays],
        in_specs=[pl.BlockSpec(memory_space=pltpu.VMEM)] * count,
        out_specs=[pl.BlockSpec(memory_space=pltpu.VMEM)] * count,
        scratch_shapes=gather_sems(n, count) + [pltpu.SemaphoreType.DMA((count,))],
        compiler_params=pltpu.CompilerParams(
            collective_id=cid, has_side_effects=True, vmem_limit_bytes=VMEM_LIMIT
        ),
        name=f"gather_{cid}",
    )(*arrays)


def lookup_kernel(
    n, vocab, ids, table, whole, parts, part_out, whole_out, parts_out, acc,
    s0, s1, s2, s3, psend, precv, local
):
    step = pl.program_id(0)
    steps = pl.num_programs(0)
    me = lax.axis_index("heads")
    gather = Gather(n, whole, whole_out, s0, s1, s2, s3)

    def exchange(d):
        dst = lax.rem(me + d, n)
        return pltpu.make_async_remote_copy(
            src_ref=parts.at[dst],
            dst_ref=parts_out.at[me],
            send_sem=psend.at[d],
            recv_sem=precv.at[d],
            device_id={"heads": dst},
            device_id_type=MESH,
        )

    def came(d):
        src = lax.rem(me + n - d, n)
        return pltpu.make_async_remote_copy(
            src_ref=parts.at[src],
            dst_ref=parts_out.at[src],
            send_sem=psend.at[d],
            recv_sem=precv.at[d],
            device_id={"heads": src},
            device_id_type=MESH,
        )

    own_whole = pltpu.make_async_copy(whole, whole_out.at[me], local.at[0])
    own_part = pltpu.make_async_copy(parts.at[me], parts_out.at[me], local.at[1])

    @pl.when(step == 0)
    def _():
        greet(n)
        gather.start()
        for d in range(1, n):
            exchange(d).start()
        own_whole.start()
        own_part.start()
        acc[...] = jnp.zeros_like(acc)

    base = step * CHUNK
    rows = lax.broadcasted_iota(jnp.int32, (CHUNK, ids.shape[1]), 0) + base
    hot = jnp.where(rows == ids[...], 1.0, 0.0).astype(jnp.bfloat16)

    @pl.when(step < steps - 1)
    def _():
        acc[...] += jnp.dot(table[...], hot, preferred_element_type=jnp.float32)

    @pl.when(step == steps - 1)
    def _():
        columns = lax.broadcasted_iota(jnp.int32, table.shape, 1) + base
        block = jnp.where(columns < vocab, table[...].astype(jnp.float32), 0.0)
        total = acc[...] + jnp.dot(
            block.astype(jnp.bfloat16), hot, preferred_element_type=jnp.float32
        )
        part_out[...] = total.astype(jnp.bfloat16)
        gather.relay()
        gather.finish()
        for d in range(1, n):
            exchange(d).wait_send()
            came(d).wait_recv()
        own_whole.wait()
        own_part.wait()


def lookup(ids, table, whole, parts, n):
    cols, vocab = table.shape
    tokens = ids.shape[1]
    anywhere = pl.BlockSpec(memory_space=pl.ANY)
    return pl.pallas_call(
        functools.partial(lookup_kernel, n, vocab),
        grid=(pl.cdiv(vocab, CHUNK),),
        out_shape=[
            jax.ShapeDtypeStruct((cols, tokens), jnp.bfloat16),
            jax.ShapeDtypeStruct((n,) + whole.shape, whole.dtype),
            jax.ShapeDtypeStruct(parts.shape, parts.dtype),
        ],
        in_specs=[
            pl.BlockSpec((1, tokens), lambda i: (0, 0)),
            pl.BlockSpec((cols, CHUNK), lambda i: (0, i)),
            anywhere,
            anywhere,
        ],
        out_specs=[pl.BlockSpec((cols, tokens), lambda i: (0, 0)), anywhere, anywhere],
        scratch_shapes=[pltpu.VMEM((cols, tokens), jnp.float32)]
        + gather_sems(n, 1)
        + [
            pltpu.SemaphoreType.DMA((n,)),
            pltpu.SemaphoreType.DMA((n,)),
            pltpu.SemaphoreType.DMA((2,)),
        ],
        compiler_params=pltpu.CompilerParams(
            collective_id=0,
            has_side_effects=True,
            vmem_limit_bytes=VMEM_LIMIT,
            dimension_semantics=("arbitrary",),
        ),
        name="lookup",
    )(ids, table, whole, parts)


def conv_rows(x, state, taps, draft):
    tokens, channels = x.shape
    x3 = x.reshape(tokens // draft, draft, channels)
    s3 = state.reshape(tokens // draft, draft, channels)
    at = lax.broadcasted_iota(jnp.int32, (1, draft, channels), 1)
    kernel = taps.shape[0] - 1
    acc = None
    for k in range(kernel):
        back = kernel - 1 - k
        seen = x3
        if back:
            seen = jnp.where(at >= back, pltpu.roll(x3, back, 1), pltpu.roll(s3, back, 1))
        term = seen * taps[k : k + 1, :][None]
        acc = term if acc is None else acc + term
    acc = (acc + taps[kernel : kernel + 1, :][None]).reshape(tokens, channels)
    return acc * (1.0 / (1.0 + jnp.exp(-acc)))


def mixer_kernel(
    draft, zx, dt, bc_t, bc_state_t, bc_taps, x_state, x_taps, heads3, accepted, gain, h0,
    u_t, ssq, h_new, c_ref, y_ref, keep_ref
):
    tokens = zx.shape[0]
    width = zx.shape[1] // 2
    states = bc_t.shape[0] // 2
    f32, bf16 = jnp.float32, jnp.bfloat16
    bc = jnp.transpose(bc_t[...].astype(f32))
    bc_state = jnp.transpose(bc_state_t[...].astype(f32))
    bcc = conv_rows(bc, bc_state, bc_taps[...], draft)
    b = bcc[:, :states].astype(bf16)
    c = bcc[:, states:].astype(bf16)
    c_ref[...] = c.astype(f32)
    zx_all = zx[...].astype(f32)
    xc = conv_rows(zx_all[:, width:], x_state[...].astype(f32), x_taps[...], draft)
    bias, rate, skip = heads3[0:1, 0:1], heads3[1:2, 0:1], heads3[2:3, 0:1]
    raw = dt[...] + bias
    step_row = jnp.maximum(raw, 0.0) + jnp.log1p(jnp.exp(-jnp.abs(raw)))
    row = lax.broadcasted_iota(jnp.int32, (tokens, tokens), 0)
    col = lax.broadcasted_iota(jnp.int32, (tokens, tokens), 1)
    same = (row // draft == col // draft) & (col <= row)
    eye = row == col
    steps_col = jnp.sum(jnp.where(eye, step_row, 0.0), axis=1, keepdims=True)
    sum_col = jnp.sum(jnp.where(same, step_row, 0.0), axis=1, keepdims=True)
    sum_row = jnp.sum(jnp.where(eye, sum_col, 0.0), axis=0, keepdims=True)
    spread = jnp.exp(jnp.where(same, (sum_row - sum_col) * rate, -1e30))
    scores = dot_nt(c, b) * spread
    xw = xc * steps_col
    y = jnp.dot(scores.astype(bf16), xw.astype(bf16), preferred_element_type=f32)

    at = lax.broadcasted_iota(jnp.int32, (tokens, 1), 0) % draft
    kept = accepted[...]
    seqs = tokens // draft
    last = jnp.where(at == kept - 1, sum_col, 0.0).reshape(seqs, draft, 1)
    last = jnp.broadcast_to(jnp.sum(last, axis=1, keepdims=True), (seqs, draft, 1))
    last = last.reshape(tokens, 1)
    coef = jnp.exp(jnp.where(at < kept, (sum_col - last) * rate, -1e30))
    keep_ref[...] = jnp.broadcast_to(jnp.exp(-last * rate), keep_ref.shape)
    xk_t = jnp.transpose(xw * coef).astype(bf16)
    lanes = 128
    in_group = lanes // draft
    group_row = lax.broadcasted_iota(jnp.int32, (lanes, states), 0) // draft
    for q in range(seqs):
        rows = slice(q * draft, (q + 1) * draft)
        g = q // in_group
        state = h0[q]
        y_ref[rows, :] = dot_nt(c_ref[rows, :].astype(bf16), state.astype(bf16))
        mine = jnp.where(
            group_row == q % in_group, b[g * lanes : (g + 1) * lanes].astype(f32), 0.0
        )
        added = jnp.dot(
            xk_t[:, g * lanes : (g + 1) * lanes],
            mine.astype(bf16),
            preferred_element_type=f32,
        )
        h_new[q] = keep_ref[q * draft : q * draft + 1, :] * state + added
    y = y + jnp.exp(-sum_col * rate) * y_ref[...] + skip * xc
    z = zx_all[:, :width]
    gated = y * (z * (1.0 / (1.0 + jnp.exp(-z))))
    u = gated * gain[...]
    u_t[...] = jnp.transpose(u).astype(bf16)
    gated_t = jnp.transpose(gated)
    ssq[...] = jnp.broadcast_to(jnp.sum(gated_t * gated_t, axis=0, keepdims=True), ssq.shape)


def mix_tokens(draft, zx, h0, *rest):
    tokens, width = zx.shape[0], zx.shape[1] // 2
    states = h0.shape[2]
    count = 2 + len(rest)
    return pl.pallas_call(
        functools.partial(mixer_kernel, draft),
        out_shape=[
            jax.ShapeDtypeStruct((width, tokens), jnp.bfloat16),
            jax.ShapeDtypeStruct((8, tokens), jnp.float32),
            jax.ShapeDtypeStruct(h0.shape, jnp.float32),
        ],
        in_specs=[pl.BlockSpec(memory_space=pltpu.VMEM)] * count,
        out_specs=[pl.BlockSpec(memory_space=pltpu.VMEM)] * 3,
        scratch_shapes=[
            pltpu.VMEM((tokens, states), jnp.float32),
            pltpu.VMEM((tokens, width), jnp.float32),
            pltpu.VMEM((tokens, states), jnp.float32),
        ],
        compiler_params=pltpu.CompilerParams(vmem_limit_bytes=VMEM_LIMIT),
        name="mixer",
    )(zx, *rest, h0)


def local(
    draft_ids, accepted, embedding, norm_gain, w_zx, w_dt, w_bc, dt_bias, decay_rate,
    skip_weight, conv_x_w, conv_x_b, conv_bc_w, conv_bc_b, gate_gain, out_w, ssm_state,
    conv_x_state, conv_bc_state,
):
    f32, bf16 = jnp.float32, jnp.bfloat16
    n = lax.axis_size("heads")
    seqs, draft = draft_ids.shape
    tokens = seqs * draft
    width = w_zx.shape[3] // 2
    own_cols = embedding.shape[1]
    model = own_cols * n
    inner = width * n
    bc_here = w_bc.shape[2]
    kernel = conv_x_w.shape[1]
    me = lax.axis_index("heads")

    rows_before = draft - (kernel - 1)
    bc_pad = jnp.pad(conv_bc_state, ((0, 0), (0, 0), (rows_before, 0), (0, 0)))
    bc_pad = bc_pad.transpose(0, 3, 1, 2).reshape(LAYERS, bc_here, tokens)
    x_pad = jnp.pad(conv_x_state, ((0, 0), (0, 0), (rows_before, 0), (0, 0)))
    x_pad = x_pad.reshape(LAYERS, tokens, width)
    bc_taps = jnp.concatenate([conv_bc_w, conv_bc_b[:, None]], axis=1).transpose(0, 2, 1)
    bc_taps = jnp.pad(bc_taps, ((0, 0), (0, 0), (0, 128 - kernel - 1)))
    x_taps = jnp.concatenate([conv_x_w, conv_x_b[:, None]], axis=1).astype(f32)
    heads3 = jnp.stack([dt_bias, decay_rate, skip_weight], axis=1)
    kept = jnp.repeat(accepted, draft)[:, None]
    w_bd = jnp.concatenate([w_bc.transpose(0, 2, 1), w_dt.transpose(0, 2, 1)], axis=1)

    parts = out_w[1].reshape(width, n, own_cols).transpose(1, 0, 2)
    part, out_whole, out_mine = lookup(
        draft_ids.reshape(1, tokens), embedding.T, out_w[0], parts, n
    )
    stream, bc_pad_all, bc_taps_all = all_gather([part, bc_pad, bc_taps], n, 1)
    stream = stream.reshape(model, tokens)
    bc_pad_all = bc_pad_all.transpose(1, 0, 2, 3).reshape(LAYERS, n * bc_here, tokens)
    bc_taps_all = bc_taps_all[..., : kernel + 1].transpose(1, 3, 0, 2)
    bc_taps_all = bc_taps_all.reshape(LAYERS, kernel + 1, n * bc_here).astype(f32)
    saved_state, saved_x, saved_bc = [], [], []
    result = None
    for layer in range(LAYERS):
        value = stream.astype(f32)
        normed = (
            value
            * rms_scale(jnp.sum(value * value, 0, keepdims=True), model)
            * norm_gain[layer][:, None]
        ).astype(bf16)
        zx = dot_tn(normed, w_zx[layer].reshape(model, -1)).astype(bf16)
        bd = jnp.dot(w_bd[layer], normed, preferred_element_type=f32).astype(bf16)
        bc_t = bd[:bc_here]
        dt = bd[bc_here:].astype(f32)
        (bc_all,) = all_gather([bc_t], n, 2 + 2 * layer)
        u_t, ssq, h_new = mix_tokens(
            draft, zx, ssm_state[layer].reshape(seqs, width, -1), dt,
            bc_all.reshape(n * bc_here, tokens), bc_pad_all[layer], bc_taps_all[layer],
            x_pad[layer], x_taps[layer], heads3[layer], kept, gate_gain[layer][None],
        )
        saved_state.append(h_new.reshape(ssm_state.shape[1:]))
        window_x = jnp.concatenate(
            [conv_x_state[layer], zx[:, width:].reshape(seqs, draft, width)], axis=1
        )
        saved_x.append(keep_rows(window_x, accepted, kernel - 1))
        window_bc = jnp.concatenate(
            [conv_bc_state[layer], bc_t.T.reshape(seqs, draft, bc_here)], axis=1
        )
        saved_bc.append(keep_rows(window_bc, accepted, kernel - 1))
        u_all, ssq_all = all_gather([u_t, ssq], n, 3 + 2 * layer)
        u_all = u_all.reshape(inner, tokens)
        scale = rms_scale(jnp.sum(ssq_all[:, 0], axis=0), inner)[None]
        if layer + 1 < LAYERS:
            mix = dot_tn(out_whole.reshape(inner, model), u_all) * scale
            stream = (value + mix).astype(bf16)
        else:
            mix = dot_tn(out_mine.reshape(inner, own_cols), u_all) * scale
            mine = lax.dynamic_slice_in_dim(stream, me * own_cols, own_cols, 0)
            result = (mine.astype(f32) + mix).astype(bf16).T
    return (result, jnp.stack(saved_state), jnp.stack(saved_x), jnp.stack(saved_bc))


def solution(mesh):
    placed = (
        P("batch", None),
        P("batch"),
        P(None, "heads"),
        P(),
        P(None, None, "heads", None),
        P(None, None, "heads"),
        P(None, None, "heads"),
        P(None, "heads"),
        P(None, "heads"),
        P(None, "heads"),
        P(None, None, "heads"),
        P(None, "heads"),
        P(None, None, "heads"),
        P(None, "heads"),
        P(None, "heads"),
        P(None, "heads", None),
        P(None, "batch", "heads", None, None),
        P(None, "batch", None, "heads"),
        P(None, "batch", None, "heads"),
    )
    return jax.shard_map(
        local,
        mesh=mesh,
        in_specs=placed,
        out_specs=(
            P("batch", "heads"),
            P(None, "batch", "heads", None, None),
            P(None, "batch", None, "heads"),
            P(None, "batch", None, "heads"),
        ),
        check_vma=False,
    )
```

profile of v0, /device:TPU:0, one launch (start us, length us, event | category | flops | bytes accessed | tf_op | source)
XLA Modules:
  0.0 181.1 jit_solution(2036383227433802943)
XLA Ops:
  0.6 0.7 copy.161
  1.4 1.3 fusion.59
  2.7 0.7 pad_maximum_fusion.7
  4.0 0.7 broadcast_compare_fusion.6
  4.7 0.7 maximum_convert_fusion
  5.4 0.6 slice_bitcast_fusion.7
  6.0 0.8 copy.154
  6.8 0.8 copy.155
  7.6 0.6 pad.13.refs_2_
  8.2 0.7 copy.158
  9.0 0.8 copy.151
  9.7 0.7 reshape.112.ids
  10.4 0.7 broadcast_in_dim.161
  11.1 0.9 slice_reduce_fusion.2
  12.1 0.8 fusion.57
  13.0 0.8 slice_bitcast_fusion.6
  13.8 0.8 pad_bitcast_fusion
  14.8 0.7 copy.156.refs_1_
  15.6 0.8 broadcast_in_dim_reshape.4.accepted
  16.4 0.8 pad_slice_fusion.2
  17.2 0.7 copy_bitcast_fusion.1
  17.9 0.8 fusion.54
  19.0 0.8 copy.204
  19.8 43.1 %lookup.1 = (bf16[320,384]{1,0:T(8,128)(2,1)}, bf16[8,64,2560]{2,1,0:T(8,128)(2,1)}, bf16[8,64,320]{2,1,0:T(8,128)(2,1)}) custom-call(s32[1,384]{1,0:T(1,128)} %reshape.112.ids, bf16[320,50280]{1,0:T(8,128)(2,1)} %bitcast.114, bf16[64,2560]{1,0:T(8,128)(2,1)} %get-tuple-element.57.whole, bf16[8,64,320]{2,1,0:T(8,128)(2,1)} %bitcast.121), custom_call_target="tpu_custom_call" | custom-call | tf_op jit(solution)/shard_map/lookup/pallas_call | solution.py:233
  62.9 36.3 %gather_1.1 = (bf16[8,320,384]{2,1,0:T(8,128)(2,1)}, bf16[8,2,32,384]{3,2,1,0:T(8,128)(2,1)}, bf16[8,2,32,128]{3,2,1,0:T(8,128)(2,1)}) custom-call(bf16[320,384]{1,0:T(8,128)(2,1)} %get-tuple-element.20.refs_0_, bf16[2,32,384]{2,1,0:T(8,128)(2,1)} %copy.156.refs_1_, bf16[2,32,128]{2,1,0:T(8,128)(2,1)} %pad.13.refs_2_), custom_call_target="tpu_custom_call" | custom-call | tf_op jit(solution)/shard_map/gather_1/pallas_call | solution.py:147
  99.2 2.0 %fusion.55 = (bf16[1,8,32,384]{3,2,0,1:T(8,128)(2,1)}, bf16[1,8,32,384]{3,2,0,1:T(8,128)(2,1)}) fusion(bf16[2,8,32,384]{3,2,0,1:T(8,128)(2,1)} %bitcast.131), kind=kLoop, calls=%fused_computation.113 | loop fusion | bytes 786432 | tf_op jit(solution)/shard_map/slice | solution.py:426
  101.2 2.0 %multiply_reduce_fusion = f32[384]{0:T(512)S(1)} fusion(bf16[8,320,384]{2,1,0:T(8,128)(2,1)} %get-tuple-element.21), kind=kLoop, calls=%fused_computation.10 | loop fusion | flops 2948736 | bytes 1967616 | tf_op jit(solution)/shard_map/reduce_sum | solution.py:416
  103.3 0.7 copy.194.bc_taps
  104.0 0.7 copy.193.bc_taps
  106.5 0.7 convolution_convert_fusion.1.zx
  107.9 0.6 slice_bitcast_fusion.10
  109.4 8.4 %gather_2.1 = bf16[8,32,384]{2,1,0:T(8,128)(2,1)} custom-call(bf16[32,384]{1,0:T(8,128)(2,1)} %get-tuple-element.69.refs_0_), custom_call_target="tpu_custom_call" | custom-call | tf_op jit(solution)/shard_map/gather_2/pallas_call | solution.py:147
  117.8 4.0 %slice_bitcast_fusion = (f32[48,64,128]{2,1,0:T(8,128)}, f32[48,64,128]{2,1,0:T(8,128)}) fusion(f32[2,48,1,64,128]{4,3,1,2,0:T(8,128)} %bitcast.118), kind=kLoop, calls=%fused_computation.12 | loop fusion | bytes 6291456 | tf_op jit(solution)/shard_map/reshape;squeeze | solution.py:425
  121.8 4.8 %mixer.2 = (bf16[64,384]{1,0:T(8,128)(2,1)}, f32[8,384]{1,0:T(8,128)}, f32[48,64,128]{2,1,0:T(8,128)}) custom-call(bf16[384,128]{1,0:T(8,128)(2,1)} %copy-done.4, f32[1,384]{1,0:T(1,128)} %slice_convert_fusion.1.dt, bf16[256,384]{1,0:T(8,128)(2,1)} %bitcast.124, bf16[256,384]{1,0:T(8,128)(2,1)} %bitcast.127, f32[5,256]{1,0:T(8,128)} %copy.193.bc_taps, ...), custom_call_target="tpu_custom_call" | custom-call | tf_op jit(solution)/shard_map/mixer/pallas_call | solution.py:353
  126.5 12.3 %gather_3.1 = (bf16[8,64,384]{2,1,0:T(8,128)(2,1)}, f32[8,8,384]{2,1,0:T(8,128)}) custom-call(bf16[64,384]{1,0:T(8,128)(2,1)} %get-tuple-element.25.refs_0_, f32[8,384]{1,0:T(8,128)} %get-tuple-element.26.refs_1_), custom_call_target="tpu_custom_call" | custom-call | tf_op jit(solution)/shard_map/gather_3/pallas_call | solution.py:147
  138.8 0.9 slice_reduce_fusion.1
  139.7 3.5 %fusion.3 = (f32[384]{0:T(512)S(1)}, bf16[2560,384]{1,0:T(8,128)(2,1)S(1)}) fusion(f32[384]{0:T(512)S(1)} %add_rsqrt_fusion.2, bf16[8,64,2560]{2,1,0:T(8,128)(2,1)} %get-tuple-element.22, bf16[8,64,384]{2,1,0:T(8,128)(2,1)} %get-tuple-element.27, bf16[2560,384]{1,0:T(8,128)(2,1)S(1)} %bitcast.115), kind=kOutput, calls=%fused_computation.6 | convolution fusion | flops 1013513856 | bytes 6949888 | tf_op jit(solution)/shard_map/dot_general | solution.py:22
  143.3 0.7 convolution_convert_fusion.2
  144.6 0.6 slice_bitcast_fusion.9
  146.0 0.7 copy.190
  146.7 2.8 %convolution_convert_fusion.zx = bf16[384,128]{1,0:T(8,128)(2,1)S(1)} fusion(bf16[2,2560,1,128]{3,1,2,0:T(8,128)(2,1)S(1)} %copy-done.9, bf16[2560,384]{1,0:T(8,128)(2,1)} %copy-done.10, f32[2560]{0:T(1024)S(1)} %get-tuple-element.52, f32[384]{0:T(512)S(1)} %add_rsqrt_fusion.1), kind=kOutput, calls=%fused_computation.19 | convolution fusion | flops 255639552 | bytes 2734080 | tf_op jit(solution)/shard_map/dot_general | solution.py:22
  149.7 0.7 pad_maximum_fusion.2
  150.4 8.3 %gather_4.1 = bf16[8,32,384]{2,1,0:T(8,128)(2,1)} custom-call(bf16[32,384]{1,0:T(8,128)(2,1)} %get-tuple-element.71.refs_0_), custom_call_target="tpu_custom_call" | custom-call | tf_op jit(solution)/shard_map/gather_4/pallas_call | solution.py:147
  158.7 4.9 %mixer.3 = (bf16[64,384]{1,0:T(8,128)(2,1)}, f32[8,384]{1,0:T(8,128)}, f32[48,64,128]{2,1,0:T(8,128)}) custom-call(bf16[384,128]{1,0:T(8,128)(2,1)} %copy-done.5, f32[1,384]{1,0:T(1,128)} %slice_convert_fusion.dt, bf16[256,384]{1,0:T(8,128)(2,1)} %bitcast.125, bf16[256,384]{1,0:T(8,128)(2,1)} %bitcast.126, f32[5,256]{1,0:T(8,128)} %copy.194.bc_taps, ...), custom_call_target="tpu_custom_call" | custom-call | tf_op jit(solution)/shard_map/mixer/pallas_call | solution.py:353
  163.6 12.2 %gather_5.1 = (bf16[8,64,384]{2,1,0:T(8,128)(2,1)}, f32[8,8,384]{2,1,0:T(8,128)}) custom-call(bf16[64,384]{1,0:T(8,128)(2,1)} %get-tuple-element.30.refs_0_, f32[8,384]{1,0:T(8,128)} %get-tuple-element.31.refs_1_), custom_call_target="tpu_custom_call" | custom-call | tf_op jit(solution)/shard_map/gather_5/pallas_call | solution.py:147
  175.9 0.9 slice_reduce_fusion
  176.8 2.2 %fusion.9 = bf16[384,320]{0,1:T(8,128)(2,1)} fusion(bf16[8,64,320]{2,1,0:T(8,128)(2,1)} %get-tuple-element.29, bf16[8,64,384]{2,1,0:T(8,128)(2,1)} %get-tuple-element.32, f32[384]{0:T(512)S(1)} %add_rsqrt_fusion, bf16[2560,384]{1,0:T(8,128)(2,1)} %copy-done.10, s32[]{:T(128)S(6)} %select_n.89), kind=kOutput, calls=%fused_computation.18 | convolution fusion | flops 126320640 | bytes 1213956 | tf_op jit(solution)/shard_map/dot_general | solution.py:22
  179.1 2.1 %maximum_bitcast_fusion = f32[2,48,1,64,128]{4,3,2,1,0:T(8,128)} fusion(f32[1,48,1,64,128]{4,3,1,2,0:T(8,128)S(1)} %bitcast.123, f32[1,48,1,64,128]{4,3,1,2,0:T(8,128)S(1)} %bitcast.122), kind=kLoop, calls=%fused_computation.11 | loop fusion | flops 786432 | bytes 6291456
  (51 shorter events, 6.5 us)
Async XLA Ops:
  0.6 17.3 %copy-start.3 = (bf16[2,64,2560]{2,1,0:T(8,128)(2,1)S(1)}, bf16[2,64,2560]{2,1,0:T(8,128)(2,1)}, u32[]{:S(2)}) copy-start(bf16[2,64,2560]{2,1,0:T(8,128)(2,1)} %param.34) | copy-start | bytes 1966084
  99.2 4.0 %copy-start.7 = (bf16[8,2,32,128]{3,2,1,0:T(8,128)(2,1)S(1)}, bf16[8,2,32,128]{3,2,1,0:T(8,128)(2,1)}, u32[]{:S(2)}) copy-start(bf16[8,2,32,128]{3,2,1,0:T(8,128)(2,1)} %get-tuple-element.24) | copy-start | bytes 393220
  99.2 5.4 %copy-start = (bf16[8,320,384]{2,1,0:T(8,128)(2,1)S(1)}, bf16[8,320,384]{2,1,0:T(8,128)(2,1)}, u32[]{:S(2)}) copy-start(bf16[8,320,384]{2,1,0:T(8,128)(2,1)} %get-tuple-element.21) | copy-start | bytes 5898244
  104.7 1.0 copy-start.6
  105.2 1.3 copy-start.8
  107.3 14.5 %copy-start.4 = (bf16[384,128]{1,0:T(8,128)(2,1)}, bf16[384,128]{1,0:T(8,128)(2,1)S(1)}, u32[]{:S(2)}) copy-start(bf16[384,128]{1,0:T(8,128)(2,1)S(1)} %convolution_convert_fusion.1.zx) | copy-start | bytes 294916
  143.2 2.0 %copy-start.10 = (bf16[2560,384]{1,0:T(8,128)(2,1)}, bf16[2560,384]{1,0:T(8,128)(2,1)S(1)}, u32[]{:S(2)}) copy-start(bf16[2560,384]{1,0:T(8,128)(2,1)S(1)} %get-tuple-element.86) | copy-start | bytes 5898244
  143.3 3.5 %copy-start.9 = (bf16[2,2560,1,128]{3,1,2,0:T(8,128)(2,1)S(1)}, bf16[2,2560,1,128]{3,1,2,0:T(8,128)(2,1)}, u32[]{:S(2)}) copy-start(bf16[2,2560,1,128]{3,1,2,0:T(8,128)(2,1)} %param.23) | copy-start | bytes 3932164
  149.5 9.2 %copy-start.5 = (bf16[384,128]{1,0:T(8,128)(2,1)}, bf16[384,128]{1,0:T(8,128)(2,1)S(1)}, u32[]{:S(2)}) copy-start(bf16[384,128]{1,0:T(8,128)(2,1)S(1)} %convolution_convert_fusion.zx) | copy-start | bytes 294916
  158.7 20.3 %copy-start.1 = (f32[48,64,128]{2,1,0:T(8,128)S(1)}, f32[48,64,128]{2,1,0:T(8,128)}, u32[]{:S(2)}) copy-start(f32[48,64,128]{2,1,0:T(8,128)} %get-tuple-element.34) | copy-start | bytes 4718596
  163.6 15.4 %copy-start.2 = (f32[48,64,128]{2,1,0:T(8,128)S(1)}, f32[48,64,128]{2,1,0:T(8,128)}, u32[]{:S(2)}) copy-start(f32[48,64,128]{2,1,0:T(8,128)} %get-tuple-element.35) | copy-start | bytes 4718596
where the time goes:
time: 183 us; the launch traced here: 181 us
  Pallas kernels  130 us (71%)
  local copies, waits for them, and re-layouts  27.6 us (15%)
  other arithmetic  11.9 us (7%)
  matrix products  10.3 us (6%)
    pallas_call x5, Pallas kernels, all_gather(): pl.pallas_call(functools.partial(ag_kernel, n, count), out_shape=[jax.Sha...  77.5 us
    pallas_call x1, Pallas kernels, lookup(): pl.pallas_call(functools.partial(lookup_kernel, n, vocab), grid=(pl.cdiv(...  43.1 us
    pallas_call x2, Pallas kernels, mix_tokens(): pl.pallas_call(functools.partial(mixer_kernel, draft), out_shape=[jax.Sha...  9.68 us
    dot_general x4, matrix products, dot_tn(): lax.dot_general(a, b, (((0,), (0,)), ((), ())), preferred_element_type=jn...  9.23 us
    unnamed x28, local copies, waits for them, and re-layouts  4.05 us
    another operation x1, local copies, waits for them, and re-layouts, local(): ssm_state[layer].reshape(seqs, width, -1)  3.96 us

commit v1 on v0

v1 whole, which is shorter than its diff:
```python
import functools

import jax
import jax.numpy as jnp
from jax import lax
from jax.experimental import pallas as pl
from jax.experimental.pallas import tpu as pltpu
from jax.sharding import PartitionSpec as P

LAYERS = 2
EPS = 1e-05
MESH = pl.DeviceIdType.MESH
LANES = 128
VMEM_LIMIT = 63 * 1024 * 1024
PROGRAM_LIMIT = 50 * 1024 * 1024
F32, BF16 = jnp.float32, jnp.bfloat16


def rms_scale(total, count):
    return lax.rsqrt(total / count + EPS)


def dot(a, b, ca=1, cb=0):
    return lax.dot_general(a, b, (((ca,), (cb,)), ((), ())), preferred_element_type=F32)


def round_up(x, m):
    return -(-x // m) * m


def silu(v):
    return v * (1.0 / (1.0 + jnp.exp(-v)))


def eye(n, dtype):
    row = lax.broadcasted_iota(jnp.int32, (n, n), 0)
    col = lax.broadcasted_iota(jnp.int32, (n, n), 1)
    return jnp.where(row == col, 1.0, 0.0).astype(dtype)


def remote(src, dst, send, recv, axis, device):
    return pltpu.make_async_remote_copy(
        src_ref=src, dst_ref=dst, send_sem=send, recv_sem=recv,
        device_id={axis: device}, device_id_type=MESH,
    )


class Place:
    def __init__(self, n, nb):
        self.n, self.nb, self.chips = n, nb, n // 2
        self.me = lax.axis_index("heads")
        self.b = lax.axis_index("batch")
        self.core = lax.rem(self.me, 2)
        self.chip = self.me // 2
        self.mate = self.me + 1 - 2 * self.core
        self.last = self.chips - 1

    def greet(self):
        barrier = pltpu.get_barrier_semaphore()
        for d in range(1, self.n):
            pl.semaphore_signal(
                barrier, inc=1, device_id={"heads": lax.rem(self.me + d, self.n)},
                device_id_type=MESH,
            )
        for k in range(1, self.nb):
            pl.semaphore_signal(
                barrier, inc=1, device_id={"batch": lax.rem(self.b + k, self.nb)},
                device_id_type=MESH,
            )
        pl.semaphore_wait(barrier, self.n + self.nb - 2)


class Line:
    def __init__(self, place, buf, sems, arrived):
        self.p, self.buf, self.sems, self.arrived = place, buf, sems, arrived

    def copy(self, kind, d, slot, device):
        ref = self.buf(slot)
        return remote(ref, ref, self.sems.at[kind, 0, d], self.sems.at[kind, 1, d], "heads", device)

    def start(self):
        p = self.p

        @pl.when(p.chip < p.last)
        def _():
            self.copy(0, 0, p.me, p.me + 2).start()

        @pl.when(p.chip > 0)
        def _():
            self.copy(1, 0, p.me, p.me - 2).start()

        self.arrived(0, p.me)

    def step(self, d):
        p = self.p

        @pl.when(p.chip >= d)
        def _():
            slot = p.me - 2 * d
            self.copy(0, d - 1, slot, slot).wait_recv()

            @pl.when(p.chip < p.last)
            def _():
                self.copy(0, d, slot, p.me + 2).start()

            self.arrived(d, slot)

        @pl.when(p.chip + d <= p.last)
        def _():
            slot = p.me + 2 * d
            self.copy(1, d - 1, slot, slot).wait_recv()

            @pl.when(p.chip > 0)
            def _():
                self.copy(1, d, slot, p.me - 2).start()

            self.arrived(p.last + d, slot)

    def each(self, fn):
        p = self.p
        fn(0, 0)
        for d in range(1, p.chips):
            @pl.when(p.chip >= d)
            def _(d=d):
                fn(d, -2 * d)

            @pl.when(p.chip + d <= p.last)
            def _(d=d):
                fn(p.last + d, 2 * d)

    def sent(self):
        p = self.p
        for d in range(p.chips - 1):
            @pl.when((p.chip >= d) & (p.chip < p.last))
            def _(d=d):
                self.copy(0, d, p.me, p.me).wait_send()

            @pl.when((p.chip + d <= p.last) & (p.chip > 0))
            def _(d=d):
                self.copy(1, d, p.me, p.me).wait_send()


class Direct:
    def __init__(self, place, out, sems):
        self.p, self.out, self.sems = place, out, sems

    def copy(self, slot, device, kind, c):
        ref = self.out.at[slot]
        return remote(ref, ref, self.sems.at[kind, 0, c], self.sems.at[kind, 1, c], "heads", device)

    def slot(self, c, core):
        p = self.p
        return 2 * lax.rem(p.chip + p.chips - c, p.chips) + core

    def order(self):
        return sorted(range(1, self.p.chips), key=lambda c: min(c, self.p.chips - c))

    def start(self):
        p = self.p
        self.copy(p.me, p.mate, 0, 0).start()
        for c in self.order():
            dst = 2 * lax.rem(p.chip + c, p.chips) + p.core
            self.copy(p.me, dst, 0, c).start()

    def relay(self):
        p = self.p
        for c in self.order():
            slot = self.slot(c, p.core)
            self.copy(slot, slot, 0, c).wait_recv()
            self.copy(slot, p.mate, 1, c).start()

    def finish(self):
        p = self.p
        self.copy(p.mate, p.mate, 0, 0).wait_recv()
        for c in range(1, p.chips):
            slot = self.slot(c, 1 - p.core)
            self.copy(slot, p.mate, 1, c).wait_recv()

    def sent(self):
        p = self.p
        for c in range(p.chips):
            self.copy(p.me, p.mate, 0, c).wait_send()
        for c in range(1, p.chips):
            self.copy(p.me, p.mate, 1, c).wait_send()


class Spread:
    def __init__(self, axis, me, n, src, dst, sems):
        self.axis, self.me, self.n = axis, me, n
        self.src, self.dst, self.sems = src, dst, sems

    def copy(self, d, peer, at):
        return remote(
            self.src(peer), self.dst(at), self.sems.at[0, d], self.sems.at[1, d], self.axis, peer
        )

    def start(self):
        for d in range(1, self.n):
            self.copy(d, lax.rem(self.me + d, self.n), self.me).start()

    def came(self):
        for d in range(1, self.n):
            peer = lax.rem(self.me + self.n - d, self.n)
            self.copy(d, peer, peer).wait_recv()

    def sent(self):
        for d in range(1, self.n):
            self.copy(d, lax.rem(self.me + d, self.n), self.me).wait_send()


def take_tokens(ids, table, tokens):
    draft, seqs = ids.shape
    rows = table.shape[0]
    lane = lax.broadcasted_iota(jnp.int32, (rows, LANES), 1)
    blocks = []
    for g in range(tokens // LANES):
        acc = jnp.zeros((rows, LANES), F32)
        at = g * LANES
        while at < (g + 1) * LANES:
            t, s0 = at // seqs, at % seqs
            count = min(seqs - s0, (g + 1) * LANES - at)
            unroll = 8
            while count % unroll:
                unroll //= 2

            def body(i, acc, t=t, s0=s0, j0=at - g * LANES, unroll=unroll):
                for k in range(unroll):
                    s = i * unroll + k
                    token = ids[t, s0 + s]
                    inside = token & (LANES - 1)
                    start = pl.multiple_of(token - inside, LANES)
                    block = table[:, pl.ds(start, LANES)].astype(F32)
                    shift = (j0 + s + LANES - inside) & (LANES - 1)
                    acc = jnp.where(lane == j0 + s, pltpu.roll(block, shift, 1), acc)
                return acc

            acc = lax.fori_loop(0, count // unroll, body, acc)
            at += count
        blocks.append(acc)
    return blocks


def split_rows(cols):
    if cols % 80:
        return [cols]
    return [cols * 2 // 5, cols * 2 // 5, cols // 5]


def lookup_kernel(cuts, vocab, *refs):
    ids, tail, table, part = refs[:4]
    tabs, sems = refs[4:-1], refs[-1]
    tokens = part.shape[1]
    full = vocab // LANES * LANES
    loads, first = [], 0
    for f, rows in enumerate(cuts):
        loads.append(
            pltpu.make_async_copy(
                table.at[pl.ds(first, rows), pl.ds(0, full)], tabs[f].at[:, pl.ds(0, full)],
                sems.at[f],
            )
        )
        loads[-1].start()
        first += rows
    first = 0
    for f, rows in enumerate(cuts):
        here = slice(first, first + rows)
        tabs[f][:, full:] = tail[here]
        loads[f].wait()
        for g, block in enumerate(take_tokens(ids, tabs[f], tokens)):
            part[here, g * LANES : (g + 1) * LANES] = block.astype(BF16)
        first += rows


def lookup(ids, table, tokens):
    cols, vocab = table.shape
    full = vocab // LANES * LANES
    cuts = split_rows(cols)
    return pl.pallas_call(
        functools.partial(lookup_kernel, cuts, vocab),
        grid=(1,),
        out_shape=jax.ShapeDtypeStruct((cols, tokens), BF16),
        in_specs=[
            pl.BlockSpec(memory_space=pltpu.SMEM),
            pl.BlockSpec((cols, LANES), lambda i: (0, full // LANES)),
            pl.BlockSpec(memory_space=pl.ANY),
        ],
        out_specs=pl.BlockSpec((cols, tokens), lambda i: (0, 0)),
        scratch_shapes=[pltpu.VMEM((rows, full + LANES), BF16) for rows in cuts]
        + [pltpu.SemaphoreType.DMA((len(cuts),))],
        compiler_params=pltpu.CompilerParams(vmem_limit_bytes=VMEM_LIMIT),
        name="lookup",
    )(ids, table, table)


def program_kernel(cfg, *refs):
    n, nb, blocks, draft = cfg
    (bias, rate_ref, skip_ref, accepted, gain, w_dt, x_w, x_b, bc_w, bc_b, gate_gain,
     x_state, bc_state, part, w_zx, w_bc, out_w, ssm,
     hidden, new_x, new_bc, h1) = refs[:22]
    refs = refs[22:]
    (stream, val, nrm, wl, gcol, wz, wb, ow, parts_src, parts, whole, bca, bcf, ua, sq, h0,
     c_s, b_s, x_s, y_s, k_s,
     load_sem, line_sems, w_line, w_batch, w_mate,
     mate_sems, bc_sems, u_sems, sq_sems, part_sems, part_batch) = refs
    p = Place(n, nb)
    me = p.me
    cols = part.shape[0]
    model = cols * n
    rows = cols // blocks
    seqs = accepted.shape[1]
    tokens = draft * seqs
    width = x_b.shape[1]
    inner = width * n
    bc_here = bc_b.shape[1]
    states = n * bc_here // 2
    kernel = x_w.shape[1]
    dt_row = 2 * width + round_up(bc_here, 16)

    small = [
        pltpu.make_async_copy(out_w.at[1, p.b], ow, load_sem.at[0]),
        pltpu.make_async_copy(out_w.at[0, p.b], whole.at[me, p.b], load_sem.at[1]),
        pltpu.make_async_copy(w_zx, wz, load_sem.at[2]),
        pltpu.make_async_copy(w_bc, wb, load_sem.at[3]),
        pltpu.make_async_copy(ssm, h0, load_sem.at[4]),
    ]
    own = pltpu.make_async_copy(part, stream.at[me], load_sem.at[5])
    own.start()
    for load in small:
        load.start()
    p.greet()

    def w_arrived(e, slot):
        block = whole.at[slot, p.b]
        for k in range(1, nb):
            remote(
                block, block, w_batch.at[0, k, e], w_batch.at[1, k, e], "batch",
                lax.rem(p.b + k, nb),
            ).start()
        remote(block, block, w_mate.at[0, 0, e], w_mate.at[1, 0, e], "heads", p.mate).start()

    w_line_g = Line(p, lambda slot: whole.at[slot, p.b], w_line, w_arrived)

    def line_of(f):
        def arrived(e, slot):
            ref = stream.at[slot, pl.ds(f * rows, rows)]
            remote(
                ref, ref, mate_sems.at[f, 0, e], mate_sems.at[f, 1, e], "heads", p.mate
            ).start()

        return Line(p, lambda slot: stream.at[slot, pl.ds(f * rows, rows)], line_sems.at[f], arrived)

    lines = [line_of(f) for f in range(blocks)]
    own.wait()
    for line in lines:
        line.start()
    small[0].wait()
    own_w = ow[...].astype(F32)
    for d in range(n):
        parts_src[d] = own_w[:, d * cols : (d + 1) * cols].astype(BF16)
    part_g = Spread(
        "heads", me, n, lambda d: parts_src.at[d], lambda d: parts.at[d, p.b], part_sems
    )

    for load in small[2:4]:
        load.wait()
    gcol[...] = jnp.transpose(jnp.concatenate([gain[...], jnp.zeros((6, model), F32)], axis=0))
    for layer in range(LAYERS):
        wl[layer, 0 : 2 * width] = jnp.transpose(wz[layer].astype(F32)).astype(BF16)
        wl[layer, 2 * width :] = jnp.zeros((wl.shape[1] - 2 * width, model), BF16)
        wl[layer, 2 * width : 2 * width + bc_here] = wb[layer]
        wl[layer, dt_row : dt_row + 1] = w_dt[layer : layer + 1, :]
    small[1].wait()
    for d in range(1, p.chips):
        for line in lines:
            line.step(d)
        if d == max(p.chips - 2, 1):
            w_line_g.start()
    for f in range(blocks):
        def landed(e, off, f=f):
            ref = stream.at[p.mate + off, pl.ds(f * rows, rows)]
            remote(
                ref, ref, mate_sems.at[f, 0, e], mate_sems.at[f, 1, e], "heads", p.mate
            ).wait_recv()

        lines[f].each(landed)

    total = jnp.zeros((1, tokens), F32)
    for i in range(n):
        v = stream[i].astype(F32)
        val[i * cols : (i + 1) * cols] = v
        total = total + jnp.sum(v * v, axis=0, keepdims=True)

    row_seq = accepted[...]
    kept = jnp.sum(
        jnp.where(eye(seqs, F32) > 0, jnp.broadcast_to(row_seq, (seqs, seqs)), 0),
        axis=1, keepdims=True,
    )
    row = lax.broadcasted_iota(jnp.int32, (tokens, tokens), 0)
    col = lax.broadcasted_iota(jnp.int32, (tokens, tokens), 1)
    same = (lax.rem(row, seqs) == lax.rem(col, seqs)) & (col <= row)
    diag = row == col

    def at(value, t):
        return value[t * seqs : (t + 1) * seqs]

    def keep_rows(window, j):
        chosen = at(window, 1 + j)
        for a in range(2, draft + 1):
            chosen = jnp.where(kept == a, at(window, a + j), chosen)
        return chosen

    def convolve(window, taps, b):
        acc = window[0:tokens] * taps[0:1].astype(F32)
        for k in range(1, kernel):
            acc = acc + window[k * seqs : k * seqs + tokens] * taps[k : k + 1].astype(F32)
        return silu(acc + b.astype(F32))

    def spread_tokens(ref, value):
        for t in range(draft):
            ref[pl.ds(t, seqs, stride=draft), :] = at(value, t)

    step_rows = model // 8
    for layer in range(LAYERS):
        scale = rms_scale(total, model)
        for i in range(8):
            here = slice(i * step_rows, (i + 1) * step_rows)
            nrm[here] = (val[here] * scale * gcol[here, layer : layer + 1]).astype(BF16)
        zb = dot(wl[layer], nrm[...]).astype(BF16).astype(F32)
        high = round_up(wl.shape[1], LANES)
        zb = jnp.concatenate([zb, jnp.zeros((high - wl.shape[1], tokens), F32)], axis=0)
        tb = jnp.transpose(zb)
        bc = tb[:, 2 * width : 2 * width + bc_here]
        eye_s = eye(seqs, BF16)
        eye_c = eye(bc_here, BF16)
        past = [dot(eye_s, bc_state[layer, j], 1, 1) for j in range(kernel - 1)]
        window_bc = jnp.concatenate(past + [bc], axis=0)
        bcc = convolve(window_bc, bc_w[layer], bc_b[layer : layer + 1])
        bca[layer, me] = dot(eye_c, bcc.astype(BF16), 1, 1).astype(BF16)
        bc_g = Direct(p, bca.at[layer], bc_sems.at[layer])
        bc_g.start()
        if layer == 0:
            w_line_g.step(1)
            part_g.start()
            parts[me, p.b] = parts_src[me]
        for j in range(kernel - 1):
            new_bc[layer, j] = dot(eye_c, keep_rows(window_bc, j).astype(BF16), 1, 1).astype(BF16)
        z = tb[:, :width]
        window_x = jnp.concatenate(
            [x_state[layer, j].astype(F32) for j in range(kernel - 1)] + [tb[:, width : 2 * width]],
            axis=0,
        )
        xc = convolve(window_x, x_w[layer], x_b[layer : layer + 1])
        for j in range(kernel - 1):
            new_x[layer, j] = keep_rows(window_x, j).astype(BF16)
        raw = tb[:, dt_row : dt_row + 1] + bias[0, layer]
        rate, skip = rate_ref[0, layer], skip_ref[0, layer]
        step = jnp.maximum(raw, 0.0) + jnp.log1p(jnp.exp(-jnp.abs(raw)))
        sums = [at(step, 0)]
        for t in range(1, draft):
            sums.append(sums[-1] + at(step, t))
        sum_col = jnp.concatenate(sums, axis=0)
        sum_row = jnp.sum(jnp.where(diag, sum_col, 0.0), axis=0, keepdims=True)
        spread = jnp.exp(jnp.where(same, (sum_row - sum_col) * rate, -1e30))
        xw = xc * step
        final = sums[0]
        for t in range(1, draft):
            final = jnp.where(kept == t + 1, sums[t], final)
        coef = jnp.concatenate(
            [jnp.exp(jnp.where(kept > t, (sums[t] - final) * rate, -1e30)) for t in range(draft)],
            axis=0,
        )
        k_s[...] = jnp.broadcast_to(jnp.exp(-final * rate), k_s.shape)
        spread_tokens(x_s, xw * coef)
        xk_t = jnp.transpose(x_s[...]).astype(BF16)
        if layer == 0:
            small[4].wait()
        bc_g.relay()
        if layer == 0:
            for d in range(2, p.chips):
                w_line_g.step(d)
        bc_g.finish()
        for i in range(n):
            bcf[i * bc_here : (i + 1) * bc_here] = bca[layer, i].astype(F32)
        bcc_all = jnp.transpose(bcf[...])
        b, c = bcc_all[:, :states], bcc_all[:, states:]
        spread_tokens(c_s, c)
        spread_tokens(b_s, b)
        scores = dot(c.astype(BF16), b.astype(BF16), 1, 1) * spread
        y = dot(scores.astype(BF16), xw.astype(BF16))
        for q in range(seqs):
            here = slice(q * draft, (q + 1) * draft)
            y_s[here] = dot(c_s[here].astype(BF16), h0[layer, q].astype(BF16), 1, 1)
        y0 = jnp.concatenate(
            [y_s[pl.ds(t, seqs, stride=draft), :] for t in range(draft)], axis=0
        )
        y = y + jnp.exp(-sum_col * rate) * y0 + skip * xc
        gated = y * silu(z)
        ua[layer, me] = jnp.transpose(gated * gate_gain[layer : layer + 1]).astype(BF16)
        gated_t = jnp.transpose(gated)
        sq[layer, me] = jnp.sum(gated_t * gated_t, axis=0, keepdims=True)
        u_g = Direct(p, ua.at[layer], u_sems.at[layer])
        u_g.start()
        sq_g = Spread(
            "heads", me, n, lambda d: sq.at[layer, me], lambda d: sq.at[layer, d],
            sq_sems.at[layer],
        )
        sq_g.start()
        if layer == 0:
            def cross(e, off):
                for k in range(1, nb):
                    block = whole.at[me + off, lax.rem(p.b + nb - k, nb)]
                    remote(
                        block, block, w_batch.at[0, k, e], w_batch.at[1, k, e], "batch", p.b
                    ).wait_recv()
                    remote(
                        block, block, w_mate.at[0, k, e], w_mate.at[1, k, e], "heads", p.mate
                    ).start()

            w_line_g.each(cross)
            part_g.came()
            part_b = Spread(
                "batch", p.b, nb, lambda d: parts.at[:, p.b], lambda d: parts.at[:, d], part_batch
            )
            part_b.start()
        in_group = LANES // draft
        group_row = lax.broadcasted_iota(jnp.int32, (LANES, states), 0) // draft
        for q in range(seqs):
            g = q // in_group
            mine = jnp.where(
                group_row == q % in_group, b_s[g * LANES : (g + 1) * LANES], 0.0
            )
            added = dot(xk_t[:, g * LANES : (g + 1) * LANES], mine.astype(BF16))
            h1[layer, q] = k_s[q : q + 1] * h0[layer, q] + added
        u_g.relay()
        u_g.finish()
        sq_g.came()
        u_all = ua[layer].reshape(inner, tokens)
        ssq = jnp.sum(sq[layer].reshape(n, tokens), axis=0, keepdims=True)
        out_scale = rms_scale(ssq, inner)
        if layer + 1 < LAYERS:
            def crossed(e, off):
                for k in range(nb):
                    block = whole.at[p.mate + off, lax.rem(p.b + nb - k, nb)]
                    remote(
                        block, block, w_mate.at[0, k, e], w_mate.at[1, k, e], "heads", p.mate
                    ).wait_recv()

            w_line_g.each(crossed)
            total = jnp.zeros((1, tokens), F32)
            lanes = 4 * LANES if model % (4 * LANES) == 0 else LANES
            for ch in range(model // lanes):
                here = slice(ch * lanes, (ch + 1) * lanes)
                w = whole[:, :, :, ch * lanes : (ch + 1) * lanes].reshape(inner, lanes)
                mix = dot(w, u_all, 0, 0) * out_scale
                v = (val[here] + mix).astype(BF16).astype(F32)
                val[here] = v
                total = total + jnp.sum(v * v, axis=0, keepdims=True)
        else:
            part_b.came()
            mix = dot(parts[...].reshape(inner, cols), u_all, 0, 0) * out_scale
            mine = val[pl.ds(pl.multiple_of(me * cols, 8), cols)]
            res = (mine + mix).astype(BF16)
            place = lax.rem(col, draft) * seqs + col // draft
            order = jnp.where(row == place, 1.0, 0.0).astype(BF16)
            hidden[...] = dot(res, order).astype(BF16)
        u_g.sent()
        sq_g.sent()
        bc_g.sent()

    for f in range(blocks):
        lines[f].sent()

        def done(e, off, f=f):
            ref = stream.at[me, pl.ds(f * rows, rows)]
            remote(
                ref, ref, mate_sems.at[f, 0, e], mate_sems.at[f, 1, e], "heads", p.mate
            ).wait_send()

        lines[f].each(done)
    w_line_g.sent()

    def w_done(e, off):
        block = whole.at[me, p.b]
        for k in range(nb):
            remote(
                block, block, w_mate.at[0, k, e], w_mate.at[1, k, e], "heads", p.mate
            ).wait_send()
        for k in range(1, nb):
            remote(
                block, block, w_batch.at[0, k, e], w_batch.at[1, k, e], "batch", p.b
            ).wait_send()

    w_line_g.each(w_done)
    part_g.sent()
    part_b.sent()


def local(
    draft_ids, accepted, embedding, norm_gain, w_zx, w_dt, w_bc, dt_bias, decay_rate,
    skip_weight, conv_x_w, conv_x_b, conv_bc_w, conv_bc_b, gate_gain, out_w, ssm_state,
    conv_x_state, conv_bc_state,
):
    n, nb = lax.axis_size("heads"), lax.axis_size("batch")
    seqs, draft = draft_ids.shape
    tokens = seqs * draft
    width = w_zx.shape[3] // 2
    vocab, cols = embedding.shape
    model = cols * n
    bc_here = w_bc.shape[2]
    states = ssm_state.shape[4]
    kernel = conv_x_w.shape[1]
    share = width // nb
    chips = n // 2
    blocks = 4 if cols % 64 == 0 else 1
    wl_rows = 2 * width + round_up(bc_here, 16) + 16

    part = lookup(draft_ids.T, embedding.T, tokens)
    args = [
        dt_bias.T, decay_rate.T, skip_weight.T, accepted.reshape(1, seqs), norm_gain,
        w_dt.reshape(LAYERS, model), conv_x_w, conv_x_b, conv_bc_w, conv_bc_b, gate_gain,
        conv_x_state.transpose(0, 2, 1, 3), conv_bc_state.transpose(0, 2, 3, 1), part,
        w_zx.reshape(LAYERS, model, 2 * width), w_bc.transpose(0, 2, 1),
        out_w.reshape(LAYERS, nb, share, model), ssm_state.reshape(LAYERS, seqs, width, states),
    ]
    smem = pl.BlockSpec(memory_space=pltpu.SMEM)
    vmem = pl.BlockSpec(memory_space=pltpu.VMEM)
    anywhere = pl.BlockSpec(memory_space=pl.ANY)
    dma = pltpu.SemaphoreType.DMA
    hidden, new_x, new_bc, new_ssm = pl.pallas_call(
        functools.partial(program_kernel, (n, nb, blocks, draft)),
        out_shape=[
            jax.ShapeDtypeStruct((cols, tokens), BF16),
            jax.ShapeDtypeStruct((LAYERS, kernel - 1, seqs, width), BF16),
            jax.ShapeDtypeStruct((LAYERS, kernel - 1, bc_here, seqs), BF16),
            pltpu.VMEM((LAYERS, seqs, width, states), F32),
        ],
        in_specs=[smem] * 3 + [vmem] * 10 + [anywhere] * 5,
        out_specs=[vmem] * 4,
        scratch_shapes=[
            pltpu.VMEM((n, cols, tokens), BF16),
            pltpu.VMEM((model, tokens), F32),
            pltpu.VMEM((model, tokens), BF16),
            pltpu.VMEM((LAYERS, wl_rows, model), BF16),
            pltpu.VMEM((model, 8), F32),
            pltpu.VMEM((LAYERS, model, 2 * width), BF16),
            pltpu.VMEM((LAYERS, bc_here, model), BF16),
            pltpu.VMEM((share, model), BF16),
            pltpu.VMEM((n, share, cols), BF16),
            pltpu.VMEM((n, nb, share, cols), BF16),
            pltpu.VMEM((n, nb, share, model), BF16),
            pltpu.VMEM((LAYERS, n, bc_here, tokens), BF16),
            pltpu.VMEM((n * bc_here, tokens), F32),
            pltpu.VMEM((LAYERS, n, width, tokens), BF16),
            pltpu.VMEM((LAYERS, n, 1, tokens), F32),
            pltpu.VMEM((LAYERS, seqs, width, states), F32),
            pltpu.VMEM((tokens, states), F32),
            pltpu.VMEM((tokens, states), F32),
            pltpu.VMEM((tokens, width), F32),
            pltpu.VMEM((tokens, width), F32),
            pltpu.VMEM((seqs, states), F32),
            dma((6,)),
            dma((blocks, 2, 2, chips)),
            dma((2, 2, chips)),
            dma((2, nb, 2 * chips)),
            dma((2, nb, 2 * chips)),
            dma((blocks, 2, 2 * chips)),
            dma((LAYERS, 2, 2, chips)),
            dma((LAYERS, 2, 2, chips)),
            dma((LAYERS, 2, n)),
            dma((2, n)),
            dma((2, nb)),
        ],
        compiler_params=pltpu.CompilerParams(
            collective_id=0, has_side_effects=True, vmem_limit_bytes=PROGRAM_LIMIT
        ),
        name="program",
    )(*args)
    return (
        hidden.T,
        new_ssm.reshape(ssm_state.shape),
        new_x.transpose(0, 2, 1, 3),
        new_bc.transpose(0, 3, 1, 2),
    )


def solution(mesh):
    placed = (
        P("batch", None),
        P("batch"),
        P(None, "heads"),
        P(),
        P(None, None, "heads", None),
        P(None, None, "heads"),
        P(None, None, "heads"),
        P(None, "heads"),
        P(None, "heads"),
        P(None, "heads"),
        P(None, None, "heads"),
        P(None, "heads"),
        P(None, None, "heads"),
        P(None, "heads"),
        P(None, "heads"),
        P(None, "heads", None),
        P(None, "batch", "heads", None, None),
        P(None, "batch", None, "heads"),
        P(None, "batch", None, "heads"),
    )
    return jax.shard_map(
        local,
        mesh=mesh,
        in_specs=placed,
        out_specs=(
            P("batch", "heads"),
            P(None, "batch", "heads", None, None),
            P(None, "batch", None, "heads"),
            P(None, "batch", None, "heads"),
        ),
        check_vma=False,
    )
```

time: 183 us -> 93.9 us (0.51)
  Pallas kernels: 130 us -> 88.1 us
  local copies, waits for them, and re-layouts: 27.6 us -> 4.61 us
  other arithmetic: 11.9 us -> 0 us
  matrix products: 10.3 us -> 0 us
    pallas_call x8 -> x2, Pallas kernels: 130 us -> 88.1 us  [the longest x1 62.9 us: local(): pl.pallas_call(functools.partial(program_kernel, (n, nb, blocks, draft)),...]
    dot_general x6 -> x0, matrix products: 10.3 us -> none  [the longest x4 9.23 us: dot_tn(): lax.dot_general(a, b, (((0,), (0,)), ((), ())), preferred_element_type=jn...]
    slice x8 -> x0, local copies, waits for them, and re-layouts: 6.59 us -> none  [the longest x1 1.95 us: local(): bc_pad_all[layer]]
    another operation x4 -> x0, local copies, waits for them, and re-layouts: 5.84 us -> none  [the longest x1 3.96 us: local(): ssm_state[layer].reshape(seqs, width, -1)]
    reduce_sum x3 -> x0, other arithmetic: 3.88 us -> none  [the longest x1 2.04 us: local(): jnp.sum(value * value, 0, keepdims=True)]
    squeeze x5 -> x0, local copies, waits for them, and re-layouts: 3.48 us -> none  [the longest x2 1.36 us: local(): bc_taps_all[layer]]
    transpose x7 -> x0, local copies, waits for them, and re-layouts: 3.18 us -> none  [the longest x4 1.47 us: local(): bc_t.T.reshape(seqs, draft, bc_here)]
    another operation x7 -> x0, other arithmetic: 2.77 us -> none  [the longest x3 1.19 us: local(): jnp.stack(saved_bc)]
where the time goes in v1:
time: 93.9 us; the launch traced here: 93.6 us
  Pallas kernels  88.1 us (94%)
  local copies, waits for them, and re-layouts  4.61 us (5%)
    pallas_call x1, Pallas kernels, local(): pl.pallas_call(functools.partial(program_kernel, (n, nb, blocks, draft)),...  62.9 us
    pallas_call x1, Pallas kernels, lookup(): pl.pallas_call(functools.partial(lookup_kernel, cuts, vocab), grid=(1,),...  25.2 us
    unnamed x32, local copies, waits for them, and re-layouts  4.61 us

profile of v1, /device:TPU:0, one launch (start us, length us, event | category | flops | bytes accessed | tf_op | source)
XLA Modules:
  0.0 93.6 jit_solution(17398416808583632423)
XLA Ops:
  0.6 0.0 copy-start.1
  0.6 0.0 copy-start.2
  0.7 0.0 copy-start.3
  0.7 0.0 copy-start.4
  0.7 0.0 copy-start.5
  0.7 0.0 copy-start.6
  0.7 0.0 copy-start.7
  0.7 0.0 copy-start.8
  0.7 0.0 copy-start.9
  0.7 0.0 copy-start.10
  0.7 0.0 copy-start.11
  0.7 0.0 copy-start.12
  0.8 0.0 copy-start.13
  0.8 25.2 %lookup.1.refs_13_ = bf16[320,384]{1,0:T(8,128)(2,1)} custom-call(s32[8,48]{1,0:T(8,128)} %bitcast.36, bf16[320,50280]{1,0:T(8,128)(2,1)} %bitcast.30, bf16[320,50280]{1,0:T(8,128)(2,1)} %bitcast.31), custom_call_target="tpu_custom_call" | custom-call | tf_op jit(solution)/shard_map/lookup/pallas_call | solution.py:278
  26.0 0.0 copy-done.1
  26.0 0.0 copy-done.2
  26.0 0.0 copy-done.3
  26.0 0.0 copy-done.4
  26.0 0.0 copy-done.5
  26.1 0.0 copy-done.6
  26.1 0.0 copy-done.7
  26.1 0.0 copy-done.8
  26.1 0.0 copy-done.9
  26.1 0.0 copy-done.10
  26.1 0.0 copy-done.11
  26.1 0.0 copy-done.12
  26.1 0.0 copy-done.13
  26.1 0.0 copy-start
  26.1 0.9 copy-done
  27.1 62.9 %program.1 = (bf16[320,384]{1,0:T(8,128)(2,1)S(1)}, bf16[2,3,48,64]{3,2,1,0:T(8,128)(2,1)S(1)}, bf16[2,3,32,48]{3,2,1,0:T(8,128)(2,1)S(1)}, f32[2,48,64,128]{3,2,1,0:T(8,128)S(1)}) custom-call(f32[1,2]{1,0:T(1,128)S(1)} %bitcast.26, f32[1,2]{1,0:T(1,128)S(1)} %bitcast.27, f32[1,2]{1,0:T(1,128)S(1)} %bitcast.28, s32[1,48]{1,0:T(1,128)S(1)} %bitcast.29, ...), custom_call_target="tpu_custom_call" | custom-call | tf_op jit(solution)/shard_map/program/pallas_call | solution.py:629
  90.0 1.7 %copy.28 = f32[2,48,1,64,128]{4,3,2,1,0:T(8,128)} copy(f32[2,48,1,64,128]{4,3,2,1,0:T(8,128)S(1)} %bitcast.19) | data formatting | bytes 6291456
  91.6 0.7 copy.29
  92.3 0.6 copy.30
  93.0 0.6 copy.31
Async XLA Ops:
  0.6 25.4 %copy-start.1 = (bf16[2,48,3,64]{3,1,2,0:T(8,128)(2,1)S(1)}, bf16[2,48,3,64]{3,1,2,0:T(8,128)(2,1)}, u32[]{:S(2)}) copy-start(bf16[2,48,3,64]{3,1,2,0:T(8,128)(2,1)} %param.36) | copy-start | bytes 110596
  0.6 25.4 %copy-start.2 = (bf16[2,48,3,32]{1,3,2,0:T(8,128)(2,1)S(1)}, bf16[2,48,3,32]{1,3,2,0:T(8,128)(2,1)}, u32[]{:S(2)}) copy-start(bf16[2,48,3,32]{1,3,2,0:T(8,128)(2,1)} %param.37) | copy-start | bytes 55300
  0.7 25.4 %copy-start.3 = (f32[2,2560]{1,0:T(2,128)S(1)}, f32[2,2560]{1,0:T(2,128)}, u32[]{:S(2)}) copy-start(f32[2,2560]{1,0:T(2,128)} %refs_4_.1) | copy-start | bytes 61444
  0.7 25.4 %copy-start.4 = (bf16[2,2560,1]{1,0,2:T(2,128)(2,1)S(1)}, bf16[2,2560,1]{1,0,2:T(2,128)(2,1)}, u32[]{:S(2)}) copy-start(bf16[2,2560,1]{1,0,2:T(2,128)(2,1)} %param.24) | copy-start | bytes 30724
  0.7 25.4 %copy-start.5 = (bf16[2,4,64]{2,1,0:T(4,128)(2,1)S(1)}, bf16[2,4,64]{2,1,0:T(4,128)(2,1)}, u32[]{:S(2)}) copy-start(bf16[2,4,64]{2,1,0:T(4,128)(2,1)} %refs_6_.1) | copy-start | bytes 3076
  0.7 25.4 %copy-start.6 = (bf16[2,4,32]{2,1,0:T(4,128)(2,1)S(1)}, bf16[2,4,32]{2,1,0:T(4,128)(2,1)}, u32[]{:S(2)}) copy-start(bf16[2,4,32]{2,1,0:T(4,128)(2,1)} %refs_8_.1) | copy-start | bytes 1540
  0.7 25.4 %copy-start.7 = (f32[2,64]{1,0:T(2,128)S(1)}, f32[2,64]{1,0:T(2,128)}, u32[]{:S(2)}) copy-start(f32[2,64]{1,0:T(2,128)} %refs_10_.1) | copy-start | bytes 1540
  0.7 25.4 %copy-start.8 = (f32[2,1]{0,1:T(1,128)S(1)}, f32[2,1]{0,1:T(1,128)}, u32[]{:S(2)}) copy-start(f32[2,1]{0,1:T(1,128)} %param.26) | copy-start | bytes 28
  0.7 25.4 %copy-start.9 = (f32[2,1]{0,1:T(1,128)S(1)}, f32[2,1]{0,1:T(1,128)}, u32[]{:S(2)}) copy-start(f32[2,1]{0,1:T(1,128)} %param.27) | copy-start | bytes 28
  0.7 25.4 %copy-start.10 = (f32[2,1]{0,1:T(1,128)S(1)}, f32[2,1]{0,1:T(1,128)}, u32[]{:S(2)}) copy-start(f32[2,1]{0,1:T(1,128)} %param.28) | copy-start | bytes 28
  0.7 25.4 %copy-start.11 = (s32[48]{0:T(128)S(1)}, s32[48]{0:T(128)}, u32[]{:S(2)}) copy-start(s32[48]{0:T(128)} %param.20) | copy-start | bytes 580
  0.7 25.4 %copy-start.12 = (bf16[2,64]{1,0:T(2,128)(2,1)S(1)}, bf16[2,64]{1,0:T(2,128)(2,1)}, u32[]{:S(2)}) copy-start(bf16[2,64]{1,0:T(2,128)(2,1)} %refs_7_.1) | copy-start | bytes 772
  0.8 25.4 %copy-start.13 = (bf16[2,32]{1,0:T(2,128)(2,1)S(1)}, bf16[2,32]{1,0:T(2,128)(2,1)}, u32[]{:S(2)}) copy-start(bf16[2,32]{1,0:T(2,128)(2,1)} %refs_9_.1) | copy-start | bytes 388
  26.1 0.9 %copy-start = (bf16[320,384]{1,0:T(8,128)(2,1)S(1)}, bf16[320,384]{1,0:T(8,128)(2,1)}, u32[]{:S(2)}) copy-start(bf16[320,384]{1,0:T(8,128)(2,1)} %lookup.1.refs_13_) | copy-start | bytes 737284

commit v2 on v1

--- a/solution.py
+++ b/solution.py
@@ -11,8 +11,8 @@
 EPS = 1e-05
 MESH = pl.DeviceIdType.MESH
 LANES = 128
-VMEM_LIMIT = 63 * 1024 * 1024
-PROGRAM_LIMIT = 50 * 1024 * 1024
+OUT_LIMIT = 8 * 1024 * 1024
+PROGRAM_LIMIT = 58 * 1024 * 1024
 F32, BF16 = jnp.float32, jnp.bfloat16
 
 
@@ -67,7 +67,9 @@
                 barrier, inc=1, device_id={"batch": lax.rem(self.b + k, self.nb)},
                 device_id_type=MESH,
             )
-        pl.semaphore_wait(barrier, self.n + self.nb - 2)
+
+    def greeted(self):
+        pl.semaphore_wait(pltpu.get_barrier_semaphore(), self.n + self.nb - 2)
 
 
 class Line:
@@ -144,44 +146,57 @@
     def __init__(self, place, out, sems):
         self.p, self.out, self.sems = place, out, sems
 
-    def copy(self, slot, device, kind, c):
+    def copy(self, slot, device, kind, e):
         ref = self.out.at[slot]
-        return remote(ref, ref, self.sems.at[kind, 0, c], self.sems.at[kind, 1, c], "heads", device)
-
-    def slot(self, c, core):
-        p = self.p
-        return 2 * lax.rem(p.chip + p.chips - c, p.chips) + core
-
-    def order(self):
-        return sorted(range(1, self.p.chips), key=lambda c: min(c, self.p.chips - c))
+        return remote(ref, ref, self.sems.at[kind, 0, e], self.sems.at[kind, 1, e], "heads", device)
+
+    def peers(self, distances, fn):
+        p = self.p
+        for d in distances:
+            @pl.when(p.chip + d <= p.last)
+            def _(d=d):
+                fn(d, 2 * d)
+
+            @pl.when(p.chip >= d)
+            def _(d=d):
+                fn(p.last + d, -2 * d)
 
     def start(self):
         p = self.p
         self.copy(p.me, p.mate, 0, 0).start()
-        for c in self.order():
-            dst = 2 * lax.rem(p.chip + c, p.chips) + p.core
-            self.copy(p.me, dst, 0, c).start()
+        self.peers(
+            range(p.last, 0, -1), lambda e, off: self.copy(p.me, p.me + off, 0, e).start()
+        )
+
+    def other(self, e):
+        last = self.p.last
+        return e + last if e <= last else e - last
 
     def relay(self):
         p = self.p
-        for c in self.order():
-            slot = self.slot(c, p.core)
-            self.copy(slot, slot, 0, c).wait_recv()
-            self.copy(slot, p.mate, 1, c).start()
+
+        def pass_on(e, off):
+            self.copy(p.me + off, p.me, 0, self.other(e)).wait_recv()
+            self.copy(p.me + off, p.mate, 1, e).start()
+
+        self.peers(range(1, p.chips), pass_on)
 
     def finish(self):
         p = self.p
         self.copy(p.mate, p.mate, 0, 0).wait_recv()
-        for c in range(1, p.chips):
-            slot = self.slot(c, 1 - p.core)
-            self.copy(slot, p.mate, 1, c).wait_recv()
+        self.peers(
+            range(1, p.chips), lambda e, off: self.copy(p.mate + off, p.mate, 1, e).wait_recv()
+        )
 
     def sent(self):
         p = self.p
-        for c in range(p.chips):
-            self.copy(p.me, p.mate, 0, c).wait_send()
-        for c in range(1, p.chips):
-            self.copy(p.me, p.mate, 1, c).wait_send()
+        self.copy(p.me, p.mate, 0, 0).wait_send()
+
+        def gone(e, off):
+            self.copy(p.me, p.mate, 0, e).wait_send()
+            self.copy(p.me, p.mate, 1, e).wait_send()
+
+        self.peers(range(1, p.chips), gone)
 
 
 class Spread:
@@ -208,106 +223,124 @@
             self.copy(d, lax.rem(self.me + d, self.n), self.me).wait_send()
 
 
-def take_tokens(ids, table, tokens):
-    draft, seqs = ids.shape
-    rows = table.shape[0]
-    lane = lax.broadcasted_iota(jnp.int32, (rows, LANES), 1)
-    blocks = []
-    for g in range(tokens // LANES):
-        acc = jnp.zeros((rows, LANES), F32)
-        at = g * LANES
-        while at < (g + 1) * LANES:
-            t, s0 = at // seqs, at % seqs
-            count = min(seqs - s0, (g + 1) * LANES - at)
-            unroll = 8
-            while count % unroll:
-                unroll //= 2
-
-            def body(i, acc, t=t, s0=s0, j0=at - g * LANES, unroll=unroll):
-                for k in range(unroll):
-                    s = i * unroll + k
-                    token = ids[t, s0 + s]
-                    inside = token & (LANES - 1)
-                    start = pl.multiple_of(token - inside, LANES)
-                    block = table[:, pl.ds(start, LANES)].astype(F32)
-                    shift = (j0 + s + LANES - inside) & (LANES - 1)
-                    acc = jnp.where(lane == j0 + s, pltpu.roll(block, shift, 1), acc)
-                return acc
-
-            acc = lax.fori_loop(0, count // unroll, body, acc)
-            at += count
-        blocks.append(acc)
-    return blocks
-
-
-def split_rows(cols):
-    if cols % 80:
-        return [cols]
-    return [cols * 2 // 5, cols * 2 // 5, cols // 5]
-
-
-def lookup_kernel(cuts, vocab, *refs):
-    ids, tail, table, part = refs[:4]
-    tabs, sems = refs[4:-1], refs[-1]
-    tokens = part.shape[1]
-    full = vocab // LANES * LANES
-    loads, first = [], 0
-    for f, rows in enumerate(cuts):
-        loads.append(
+class Lookup:
+    def __init__(self, ids, tail, table, tabs, pick, tiles, sems, rows):
+        self.ids, self.tail, self.table, self.tabs = ids, tail, table, tabs
+        self.pick, self.tiles, self.sems, self.rows = pick, tiles, sems, rows
+        self.full = table.shape[1] // LANES
+
+    def tab(self, f):
+        return self.tabs[f % len(self.tabs)]
+
+    def load(self, f):
+        here = pl.ds(f * self.rows, self.rows)
+
+        def one(i, carry):
             pltpu.make_async_copy(
-                table.at[pl.ds(first, rows), pl.ds(0, full)], tabs[f].at[:, pl.ds(0, full)],
-                sems.at[f],
+                self.table.at[here, pl.ds(pl.multiple_of(i * LANES, LANES), LANES)],
+                self.tab(f).at[i], self.sems.at[f],
+            ).start()
+            return carry
+
+        lax.fori_loop(0, self.full, one, 0, unroll=8 if self.full % 8 == 0 else 1)
+
+    def build(self, at, place):
+        seqs = self.ids.shape[1]
+        token = self.ids[at // seqs, lax.rem(at, seqs)]
+        row = lax.broadcasted_iota(jnp.int32, (LANES, LANES), 0)
+        col = lax.broadcasted_iota(jnp.int32, (LANES, LANES), 1)
+        self.tiles[at] = token >> 7
+        one = (row == (token & (LANES - 1))) & (col == (at & (LANES - 1)))
+        here = pl.ds(pl.multiple_of(place * LANES, LANES), LANES)
+        self.pick[here, :] = jnp.where(one, 1.0, 0.0).astype(BF16)
+
+    def prepare(self):
+        if self.pick.shape[0] == LANES * LANES:
+            return
+        draft, seqs = self.ids.shape
+        row = lax.broadcasted_iota(jnp.int32, (LANES, LANES), 0)
+        col = lax.broadcasted_iota(jnp.int32, (LANES, LANES), 1)
+        for t in range(draft):
+            def build(s, carry, t=t):
+                at = t * seqs + s
+                token = self.ids[t, s]
+                self.tiles[at] = token >> 7
+                one = (row == (token & (LANES - 1))) & (col == (at & (LANES - 1)))
+                here = pl.ds(pl.multiple_of(at * LANES, LANES), LANES)
+                self.pick[here, :] = jnp.where(one, 1.0, 0.0).astype(BF16)
+                return carry
+
+            lax.fori_loop(0, seqs, build, 0, unroll=8 if seqs % 8 == 0 else 1)
+
+    def take(self, f, put):
+        tab = self.tab(f)
+        whole = tab.at[pl.ds(0, self.full)]
+        pltpu.make_async_copy(whole, whole, self.sems.at[f]).wait()
+        tab[self.full] = self.tail[f * self.rows : (f + 1) * self.rows]
+
+        grouped = self.pick.shape[0] == LANES * LANES
+
+        def group(g, carry):
+            if grouped:
+                def build(k, inner):
+                    self.build(g * LANES + k, k)
+                    return inner
+
+                lax.fori_loop(0, LANES, build, 0)
+            found = jnp.concatenate(
+                [tab[self.tiles[g * LANES + k]] for k in range(LANES)], axis=1
             )
-        )
-        loads[-1].start()
-        first += rows
-    first = 0
-    for f, rows in enumerate(cuts):
-        here = slice(first, first + rows)
-        tabs[f][:, full:] = tail[here]
-        loads[f].wait()
-        for g, block in enumerate(take_tokens(ids, tabs[f], tokens)):
-            part[here, g * LANES : (g + 1) * LANES] = block.astype(BF16)
-        first += rows
-
-
-def lookup(ids, table, tokens):
-    cols, vocab = table.shape
-    full = vocab // LANES * LANES
-    cuts = split_rows(cols)
+            first = 0 if grouped else pl.multiple_of(g * LANES * LANES, LANES)
+            here = pl.ds(first, LANES * LANES)
+            put(g, dot(found, self.pick[here, :]).astype(BF16))
+            return carry
+
+        draft, seqs = self.ids.shape
+        lax.fori_loop(0, draft * seqs // LANES, group, 0)
+
+
+def out_kernel(*refs):
+    count = len(refs) // 2
+    sems = refs[-1]
+    copies = [
+        pltpu.make_async_copy(refs[i], refs[count + i], sems.at[i]) for i in range(count)
+    ]
+    for copy in copies:
+        copy.start()
+    for copy in copies:
+        copy.wait()
+
+
+def put_out(arrays):
+    count = len(arrays)
     return pl.pallas_call(
-        functools.partial(lookup_kernel, cuts, vocab),
-        grid=(1,),
-        out_shape=jax.ShapeDtypeStruct((cols, tokens), BF16),
-        in_specs=[
-            pl.BlockSpec(memory_space=pltpu.SMEM),
-            pl.BlockSpec((cols, LANES), lambda i: (0, full // LANES)),
-            pl.BlockSpec(memory_space=pl.ANY),
-        ],
-        out_specs=pl.BlockSpec((cols, tokens), lambda i: (0, 0)),
-        scratch_shapes=[pltpu.VMEM((rows, full + LANES), BF16) for rows in cuts]
-        + [pltpu.SemaphoreType.DMA((len(cuts),))],
-        compiler_params=pltpu.CompilerParams(vmem_limit_bytes=VMEM_LIMIT),
-        name="lookup",
-    )(ids, table, table)
+        out_kernel,
+        out_shape=[jax.ShapeDtypeStruct(a.shape, a.dtype) for a in arrays],
+        in_specs=[pl.BlockSpec(memory_space=pltpu.VMEM)] * count,
+        out_specs=[pl.BlockSpec(memory_space=pl.ANY)] * count,
+        scratch_shapes=[pltpu.SemaphoreType.DMA((count,))],
+        compiler_params=pltpu.CompilerParams(vmem_limit_bytes=OUT_LIMIT),
+        name="put_out",
+    )(*arrays)
 
 
 def program_kernel(cfg, *refs):
-    n, nb, blocks, draft = cfg
-    (bias, rate_ref, skip_ref, accepted, gain, w_dt, x_w, x_b, bc_w, bc_b, gate_gain,
-     x_state, bc_state, part, w_zx, w_bc, out_w, ssm,
-     hidden, new_x, new_bc, h1) = refs[:22]
-    refs = refs[22:]
-    (stream, val, nrm, wl, gcol, wz, wb, ow, parts_src, parts, whole, bca, bcf, ua, sq, h0,
+    n, nb, blocks = cfg
+    (ids, tail, table, bias, rate_ref, skip_ref, accepted, gain, w_dt, x_w, x_b, bc_w, bc_b, gate_gain,
+     x_state, bc_state, w_zx, w_bc, out_w, ssm,
+     hidden, new_x, new_bc, h1) = refs[:24]
+    slots = min(blocks, 3)
+    tabs, refs = refs[24 : 24 + slots], refs[24 + slots :]
+    (pick, tiles, table_sem, stream, val, nrm, wl, gcol, wz, wb, ow, parts_src, parts, whole, bca, bcf, ua, sq,
      c_s, b_s, x_s, y_s, k_s,
      load_sem, line_sems, w_line, w_batch, w_mate,
      mate_sems, bc_sems, u_sems, sq_sems, part_sems, part_batch) = refs
     p = Place(n, nb)
     me = p.me
-    cols = part.shape[0]
+    cols = table.shape[0]
     model = cols * n
     rows = cols // blocks
-    seqs = accepted.shape[1]
+    draft, seqs = ids.shape
     tokens = draft * seqs
     width = x_b.shape[1]
     inner = width * n
@@ -321,13 +354,18 @@
         pltpu.make_async_copy(out_w.at[0, p.b], whole.at[me, p.b], load_sem.at[1]),
         pltpu.make_async_copy(w_zx, wz, load_sem.at[2]),
         pltpu.make_async_copy(w_bc, wb, load_sem.at[3]),
-        pltpu.make_async_copy(ssm, h0, load_sem.at[4]),
+        pltpu.make_async_copy(ssm, h1, load_sem.at[4]),
     ]
-    own = pltpu.make_async_copy(part, stream.at[me], load_sem.at[5])
-    own.start()
-    for load in small:
+    find = Lookup(ids, tail, table, tabs, pick, tiles, table_sem, rows)
+    p.greet()
+    for load in small[:2]:
         load.start()
-    p.greet()
+    ahead = min(slots, 2)
+    for f in range(ahead):
+        find.load(f)
+    for load in small[2:]:
+        load.start()
+    p.greeted()
 
     def w_arrived(e, slot):
         block = whole.at[slot, p.b]
@@ -350,9 +388,9 @@
         return Line(p, lambda slot: stream.at[slot, pl.ds(f * rows, rows)], line_sems.at[f], arrived)
 
     lines = [line_of(f) for f in range(blocks)]
-    own.wait()
-    for line in lines:
-        line.start()
+    small[1].wait()
+    w_line_g.start()
+    find.prepare()
     small[0].wait()
     own_w = ow[...].astype(F32)
     for d in range(n):
@@ -361,20 +399,31 @@
         "heads", me, n, lambda d: parts_src.at[d], lambda d: parts.at[d, p.b], part_sems
     )
 
-    for load in small[2:4]:
-        load.wait()
-    gcol[...] = jnp.transpose(jnp.concatenate([gain[...], jnp.zeros((6, model), F32)], axis=0))
-    for layer in range(LAYERS):
-        wl[layer, 0 : 2 * width] = jnp.transpose(wz[layer].astype(F32)).astype(BF16)
-        wl[layer, 2 * width :] = jnp.zeros((wl.shape[1] - 2 * width, model), BF16)
-        wl[layer, 2 * width : 2 * width + bc_here] = wb[layer]
-        wl[layer, dt_row : dt_row + 1] = w_dt[layer : layer + 1, :]
-    small[1].wait()
-    for d in range(1, p.chips):
-        for line in lines:
-            line.step(d)
-        if d == max(p.chips - 2, 1):
-            w_line_g.start()
+    for wave in range(blocks + p.chips - 1):
+        if wave < blocks:
+            def put(g, block, f=wave):
+                at = pl.ds(pl.multiple_of(g * LANES, LANES), LANES)
+                stream[me, pl.ds(f * rows, rows), at] = block
+
+            find.take(wave, put)
+            lines[wave].start()
+            if wave + ahead < blocks:
+                find.load(wave + ahead)
+        for f in range(blocks):
+            d = wave - f
+            if 1 <= d < p.chips:
+                lines[f].step(d)
+        if 1 <= wave < p.last:
+            w_line_g.step(wave)
+        if wave == blocks - 1:
+            for load in small[2:4]:
+                load.wait()
+            gcol[...] = jnp.transpose(jnp.concatenate([gain[...], jnp.zeros((6, model), F32)], axis=0))
+            for layer in range(LAYERS):
+                wl[layer, 0 : 2 * width] = jnp.transpose(wz[layer].astype(F32)).astype(BF16)
+                wl[layer, 2 * width :] = jnp.zeros((wl.shape[1] - 2 * width, model), BF16)
+                wl[layer, 2 * width : 2 * width + bc_here] = wb[layer]
+                wl[layer, dt_row : dt_row + 1] = w_dt[layer : layer + 1, :]
     for f in range(blocks):
         def landed(e, off, f=f):
             ref = stream.at[p.mate + off, pl.ds(f * rows, rows)]
@@ -439,7 +488,6 @@
         bc_g = Direct(p, bca.at[layer], bc_sems.at[layer])
         bc_g.start()
         if layer == 0:
-            w_line_g.step(1)
             part_g.start()
             parts[me, p.b] = parts_src[me]
         for j in range(kernel - 1):
@@ -476,8 +524,7 @@
             small[4].wait()
         bc_g.relay()
         if layer == 0:
-            for d in range(2, p.chips):
-                w_line_g.step(d)
+            w_line_g.step(p.last)
         bc_g.finish()
         for i in range(n):
             bcf[i * bc_here : (i + 1) * bc_here] = bca[layer, i].astype(F32)
@@ -489,7 +536,7 @@
         y = dot(scores.astype(BF16), xw.astype(BF16))
         for q in range(seqs):
             here = slice(q * draft, (q + 1) * draft)
-            y_s[here] = dot(c_s[here].astype(BF16), h0[layer, q].astype(BF16), 1, 1)
+            y_s[here] = dot(c_s[here].astype(BF16), h1[layer, q].astype(BF16), 1, 1)
         y0 = jnp.concatenate(
             [y_s[pl.ds(t, seqs, stride=draft), :] for t in range(draft)], axis=0
         )
@@ -530,7 +577,7 @@
                 group_row == q % in_group, b_s[g * LANES : (g + 1) * LANES], 0.0
             )
             added = dot(xk_t[:, g * LANES : (g + 1) * LANES], mine.astype(BF16))
-            h1[layer, q] = k_s[q : q + 1] * h0[layer, q] + added
+            h1[layer, q] = k_s[q : q + 1] * h1[layer, q] + added
         u_g.relay()
         u_g.finish()
         sq_g.came()
@@ -614,11 +661,14 @@
     blocks = 4 if cols % 64 == 0 else 1
     wl_rows = 2 * width + round_up(bc_here, 16) + 16
 
-    part = lookup(draft_ids.T, embedding.T, tokens)
+    table = embedding.T
+    vocab = table.shape[1]
+    full = vocab // LANES
+    slots = min(blocks, 3)
     args = [
-        dt_bias.T, decay_rate.T, skip_weight.T, accepted.reshape(1, seqs), norm_gain,
+        draft_ids.T, table, table, dt_bias.T, decay_rate.T, skip_weight.T, accepted.reshape(1, seqs), norm_gain,
         w_dt.reshape(LAYERS, model), conv_x_w, conv_x_b, conv_bc_w, conv_bc_b, gate_gain,
-        conv_x_state.transpose(0, 2, 1, 3), conv_bc_state.transpose(0, 2, 3, 1), part,
+        conv_x_state.transpose(0, 2, 1, 3), conv_bc_state.transpose(0, 2, 3, 1),
         w_zx.reshape(LAYERS, model, 2 * width), w_bc.transpose(0, 2, 1),
         out_w.reshape(LAYERS, nb, share, model), ssm_state.reshape(LAYERS, seqs, width, states),
     ]
@@ -626,17 +676,23 @@
     vmem = pl.BlockSpec(memory_space=pltpu.VMEM)
     anywhere = pl.BlockSpec(memory_space=pl.ANY)
     dma = pltpu.SemaphoreType.DMA
-    hidden, new_x, new_bc, new_ssm = pl.pallas_call(
-        functools.partial(program_kernel, (n, nb, blocks, draft)),
+    results = pl.pallas_call(
+        functools.partial(program_kernel, (n, nb, blocks)),
+        grid=(1,),
         out_shape=[
-            jax.ShapeDtypeStruct((cols, tokens), BF16),
-            jax.ShapeDtypeStruct((LAYERS, kernel - 1, seqs, width), BF16),
-            jax.ShapeDtypeStruct((LAYERS, kernel - 1, bc_here, seqs), BF16),
+            pltpu.VMEM((cols, tokens), BF16),
+            pltpu.VMEM((LAYERS, kernel - 1, seqs, width), BF16),
+            pltpu.VMEM((LAYERS, kernel - 1, bc_here, seqs), BF16),
             pltpu.VMEM((LAYERS, seqs, width, states), F32),
         ],
-        in_specs=[smem] * 3 + [vmem] * 10 + [anywhere] * 5,
+        in_specs=[smem, pl.BlockSpec((cols, LANES), lambda i: (0, full)), anywhere]
+        + [smem] * 3 + [vmem] * 10 + [anywhere] * 4,
         out_specs=[vmem] * 4,
-        scratch_shapes=[
+        scratch_shapes=[pltpu.VMEM((full + 1, cols // blocks, LANES), BF16)] * slots
+        + [
+            pltpu.VMEM(((tokens if blocks > 1 else LANES) * LANES, LANES), BF16),
+            pltpu.SMEM((tokens,), jnp.int32),
+            dma((blocks,)),
             pltpu.VMEM((n, cols, tokens), BF16),
             pltpu.VMEM((model, tokens), F32),
             pltpu.VMEM((model, tokens), BF16),
@@ -652,7 +708,6 @@
             pltpu.VMEM((n * bc_here, tokens), F32),
             pltpu.VMEM((LAYERS, n, width, tokens), BF16),
             pltpu.VMEM((LAYERS, n, 1, tokens), F32),
-            pltpu.VMEM((LAYERS, seqs, width, states), F32),
             pltpu.VMEM((tokens, states), F32),
             pltpu.VMEM((tokens, states), F32),
             pltpu.VMEM((tokens, width), F32),
@@ -664,8 +719,8 @@
             dma((2, nb, 2 * chips)),
             dma((2, nb, 2 * chips)),
             dma((blocks, 2, 2 * chips)),
-            dma((LAYERS, 2, 2, chips)),
-            dma((LAYERS, 2, 2, chips)),
+            dma((LAYERS, 2, 2, 2 * chips)),
+            dma((LAYERS, 2, 2, 2 * chips)),
             dma((LAYERS, 2, n)),
             dma((2, n)),
             dma((2, nb)),
@@ -675,6 +730,7 @@
         ),
         name="program",
     )(*args)
+    hidden, new_x, new_bc, new_ssm = put_out(results)
     return (
         hidden.T,
         new_ssm.reshape(ssm_state.shape),

time: 93.9 us -> 76.1 us (0.81)
  Pallas kernels: 88.1 us -> 75.1 us
  local copies, waits for them, and re-layouts: 4.61 us -> 0 us
    pallas_call x2, Pallas kernels: 88.1 us -> 75.1 us  [the longest x1 73.3 us: local(): pl.pallas_call(functools.partial(program_kernel, (n, nb, blocks)), grid=(...]
    unnamed x32 -> x0, local copies, waits for them, and re-layouts: 4.61 us -> none
where the time goes in v2:
time: 76.1 us; the launch traced here: 75.9 us
  Pallas kernels  75.1 us (99%)
  between operations  0.81 us (1%)
    pallas_call x1, Pallas kernels, local(): pl.pallas_call(functools.partial(program_kernel, (n, nb, blocks)), grid=(...  73.3 us
    pallas_call x1, Pallas kernels, put_out(): pl.pallas_call(out_kernel, out_shape=[jax.ShapeDtypeStruct(a.shape, a.dty...  1.82 us

profile of v2, /device:TPU:0, one launch (start us, length us, event | category | flops | bytes accessed | tf_op | source)
XLA Modules:
  0.0 75.9 jit_solution(18070160185131193686)
XLA Ops:
  0.6 73.3 %program.1 = (bf16[320,384]{1,0:T(8,128)(2,1)S(1)}, bf16[2,3,48,64]{3,2,1,0:T(8,128)(2,1)S(1)}, bf16[2,3,32,48]{3,2,1,0:T(8,128)(2,1)S(1)}, f32[2,48,64,128]{3,2,1,0:T(8,128)S(1)}) custom-call(s32[8,48]{1,0:T(8,128)} %bitcast.28, bf16[320,50280]{1,0:T(8,128)(2,1)} %bitcast.19, bf16[320,50280]{1,0:T(8,128)(2,1)} %bitcast.20, f32[1,2]{1,0:T(1,128)} %bitcast.29, ...), custom_call_target="tpu_custom_call" | custom-call | tf_op jit(solution)/shard_map/program/pallas_call | solution.py:679
  73.9 1.8 %put_out.1 = (bf16[320,384]{1,0:T(8,128)(2,1)}, bf16[2,3,48,64]{3,2,1,0:T(8,128)(2,1)}, bf16[2,3,32,48]{3,2,1,0:T(8,128)(2,1)}, f32[2,48,64,128]{3,2,1,0:T(8,128)}) custom-call(bf16[320,384]{1,0:T(8,128)(2,1)S(1)} %get-tuple-element.12.refs_0_, bf16[2,3,48,64]{3,2,1,0:T(8,128)(2,1)S(1)} %get-tuple-element.13.refs_1_, ...), custom_call_target="tpu_custom_call" | custom-call | tf_op jit(solution)/shard_map/put_out/pallas_call | solution.py:316
